TPU v7x, 32 devices: a whole 2x2x4 slice. The times are simulated.
32 devices in a mesh: shard: 4 (over z), ctx: 2 (over x), tp: 4 (over y, core).
Axes of the slice: x: 2, y: 2, z: 4, core: 2. Of those that a mesh axis runs over, the one named last changes fastest.
Arguments:
- tokens: bfloat16 [8, 1024, 1280], P('shard', ('ctx', 'tp')), may hold values from -6 to 6
- norm1_gain: float32 [1280], replicated, may hold values from 0.1 to 1.9
- norm1_bias: float32 [1280], replicated, may hold values from -3 to 3
- qkv_weight: bfloat16 [3, 1280, 1280], P(None, ('shard', 'ctx'), 'tp'), may hold values from -0.15625 to 0.15625
- qv_bias: float32 [2, 1280], replicated, may hold values from -3 to 3
- rel_rows: bfloat16 [31, 80], replicated, may hold values from -0.8984375 to 0.8984375
- rel_cols: bfloat16 [127, 80], replicated, may hold values from -0.8984375 to 0.8984375
- proj_weight: bfloat16 [1280, 1280], P('tp', ('shard', 'ctx')), may hold values from -1.25 to 1.25
- proj_bias: float32 [1280], replicated, may hold values from -3 to 3
- norm2_gain: float32 [1280], replicated, may hold values from 0.1 to 1.9
- norm2_bias: float32 [1280], replicated, may hold values from -3 to 3
- fc1_weight: bfloat16 [1280, 5120], P(('shard', 'ctx'), 'tp'), may hold values from -0.15625 to 0.15625
- fc1_bias: float32 [5120], replicated, may hold values from -3 to 3
- fc2_weight: bfloat16 [5120, 1280], P('tp', ('shard', 'ctx')), may hold values from -0.078125 to 0.078125
- fc2_bias: float32 [1280], replicated, may hold values from -3 to 3
- cotangent: bfloat16 [8, 1024, 1280], P('shard', ('ctx', 'tp')), may hold values from -6 to 6
Outputs:
- output: bfloat16 [8, 1024, 1280], P('shard', ('ctx', 'tp'))
- tokens_grad: bfloat16 [8, 1024, 1280], P('shard', ('ctx', 'tp'))
- norm1_gain_grad: float32 [1280], replicated
- norm1_bias_grad: float32 [1280], replicated
- qkv_weight_grad: float32 [3, 1280, 1280], P(None, ('shard', 'ctx'), 'tp')
- qv_bias_grad: float32 [2, 1280], replicated
- rel_rows_grad: float32 [31, 80], replicated
- rel_cols_grad: float32 [127, 80], replicated
- proj_weight_grad: float32 [1280, 1280], P('tp', ('shard', 'ctx'))
- proj_bias_grad: float32 [1280], replicated
- norm2_gain_grad: float32 [1280], replicated
- norm2_bias_grad: float32 [1280], replicated
- fc1_weight_grad: float32 [1280, 5120], P(('shard', 'ctx'), 'tp')
- fc1_bias_grad: float32 [5120], replicated
- fc2_weight_grad: float32 [5120, 1280], P('tp', ('shard', 'ctx'))
- fc2_bias_grad: float32 [1280], replicated
All inputs are finite; a program needn't handle non-finite values.
Results may differ from a plain program's by a relative error of at most 0.02.
Values may be sent and summed in bfloat16 or wider, within the bound.
A program may use at most 128 MiB of HBM per device.

v0:
```python
from functools import partial
import math

import jax
import jax.numpy as jnp
from jax import lax
from jax.experimental import pallas as pl
from jax.experimental.pallas import tpu as pltpu
from jax.sharding import PartitionSpec as P

D = 1280
H = 16
HD = 80
FF = 5120
COLS = 64
ROWS_DEV = 8


PRECISE = lax.Precision.HIGHEST
EPSILON = 1e-06
NEGATIVE = -1e30


def layer_norm(values_in, gain_vec, shift_vec):
    average = jnp.mean(values_in, -1, keepdims=True)
    centred = values_in - average
    variance = jnp.mean(centred * centred, -1, keepdims=True)
    return centred * lax.rsqrt(variance + EPSILON) * gain_vec + shift_vec


def block_size():
    return 512


def to_heads(flat_rows, heads_local):
    images, length, feat_width = flat_rows.shape
    return flat_rows.reshape(images, length, heads_local, feat_width // heads_local).transpose(
        0, 2, 1, 3
    )


def from_heads(per_head):
    images, heads_local, length, head_dim = per_head.shape
    return per_head.transpose(0, 2, 1, 3).reshape(images, length, heads_local * head_dim)


def block_scores(query_heads, key_flat, rows_bias, cols_bias, first_key, scale_factor):
    key_heads = to_heads(key_flat, query_heads.shape[1])
    key_len = key_flat.shape[1]
    key_rows = key_len // COLS
    scores = scale_factor * jnp.einsum(
        "ihqc,ihkc->ihqk", query_heads, key_heads, preferred_element_type=jnp.float32
    )
    images, heads_local, query_len, unused_len = scores.shape
    row_part = lax.dynamic_slice_in_dim(rows_bias, first_key // COLS, key_rows, 3)
    scores = scores.reshape(images, heads_local, query_len, key_rows, COLS)
    scores = scores + row_part[..., :, None] + cols_bias[..., None, :]
    return scores.reshape(images, heads_local, query_len, key_len)


def relative_terms(query_flat, rows_param, cols_param, first_row, heads_local):
    images, length, feat_width = query_flat.shape
    rows_dev = length // COLS
    grid_rows = (rows_param.shape[0] + 1) // 2
    own_rows = first_row + jnp.arange(rows_dev, dtype=jnp.int32)
    key_rows = jnp.arange(grid_rows, dtype=jnp.int32)
    row_slots = jnp.arange(rows_param.shape[0], dtype=jnp.int32)
    pick_rows = (
        row_slots[None, None, :]
        == own_rows[:, None, None] - key_rows[None, :, None] + grid_rows - 1
    ).astype(jnp.float32)
    table_rows = jnp.einsum("rkj,jc->rkc", pick_rows, rows_param, precision=PRECISE)
    col_ids = jnp.arange(COLS, dtype=jnp.int32)
    col_slots = jnp.arange(cols_param.shape[0], dtype=jnp.int32)
    pick_cols = (
        col_slots[None, None, :] == col_ids[:, None, None] - col_ids[None, :, None] + COLS - 1
    ).astype(jnp.float32)
    table_cols = jnp.einsum("wkj,jc->wkc", pick_cols, cols_param, precision=PRECISE)
    grid_form = query_flat.reshape(images, rows_dev, COLS, heads_local, feat_width // heads_local)
    along_rows = jnp.einsum("irwhc,rkc->ihrwk", grid_form, table_rows, precision=PRECISE).reshape(
        images, heads_local, length, grid_rows
    )
    along_cols = jnp.einsum("irwhc,wkc->ihrwk", grid_form, table_cols, precision=PRECISE).reshape(
        images, heads_local, length, COLS
    )
    return (along_rows, along_cols)


def on_device_rows(
    tokens,
    norm1_gain,
    norm1_bias,
    qkv_weight,
    qv_bias,
    rel_rows,
    rel_cols,
    proj_weight,
    proj_bias,
    norm2_gain,
    norm2_bias,
    fc1_weight,
    fc1_bias,
    fc2_weight,
    fc2_bias,
    cotangent,
):
    scale_factor = HD ** (-0.5)
    tp_count = lax.axis_size("tp")
    ctx_count = lax.axis_size("ctx")
    tp_rank = lax.axis_index("tp")
    ctx_rank = lax.axis_index("ctx")
    grid_rows = ROWS_DEV * ctx_count
    tok_image = grid_rows * COLS
    tok_ctx = ROWS_DEV * COLS
    heads_local = H // tp_count
    width_local = heads_local * HD
    ff_local = FF // tp_count
    images = tokens.shape[0]
    rows_table = rel_rows.astype(jnp.float32)
    cols_table = rel_cols.astype(jnp.float32)
    qkv_full, proj_full, fc1_full, fc2_full = (
        lax.all_gather(qkv_weight, ("shard", "ctx"), axis=1, tiled=True),
        lax.all_gather(proj_weight, ("shard", "ctx"), axis=1, tiled=True),
        lax.all_gather(fc1_weight, ("shard", "ctx"), axis=0, tiled=True),
        lax.all_gather(fc2_weight, ("shard", "ctx"), axis=1, tiled=True),
    )
    qv_local = lax.dynamic_slice_in_dim(qv_bias, tp_rank * width_local, width_local, 1)
    fc1_local = lax.dynamic_slice_in_dim(fc1_bias, tp_rank * ff_local, ff_local, 0)
    resid_in = tokens.astype(jnp.float32)
    normed1 = layer_norm(resid_in, norm1_gain, norm1_bias).astype(jnp.bfloat16)
    normed1_full = lax.all_gather(normed1, "tp", axis=1, tiled=True)
    projected = jnp.einsum(
        "itd,sde->itse", normed1_full, qkv_full, preferred_element_type=jnp.float32
    )
    queries = (projected[:, :, 0] + qv_local[0]).astype(jnp.bfloat16)
    keys_own = projected[:, :, 1].astype(jnp.bfloat16)
    values_own = (projected[:, :, 2] + qv_local[1]).astype(jnp.bfloat16)
    first_row = ctx_rank * ROWS_DEV
    rel_fn = partial(relative_terms, first_row=first_row, heads_local=heads_local)
    (along_rows, along_cols), rel_pull = jax.vjp(
        rel_fn, queries.astype(jnp.float32), rows_table, cols_table
    )
    query_heads = to_heads(queries, heads_local)
    start_state = (
        jnp.full((images, heads_local, tok_ctx), NEGATIVE, jnp.float32),
        jnp.zeros((images, heads_local, tok_ctx), jnp.float32),
        jnp.zeros((images, heads_local, tok_ctx, HD), jnp.float32),
        jnp.zeros((images, tok_image, width_local), jnp.bfloat16),
        jnp.zeros((images, tok_image, width_local), jnp.bfloat16),
    )
    shard_piece = (
        lax.all_gather(keys_own, "ctx", axis=1, tiled=True),
        lax.all_gather(values_own, "ctx", axis=1, tiled=True),
    )
    piece_len = shard_piece[0].shape[1]
    step_len = block_size()

    def one_step(inner, offset):
        run_max, run_sum, run_acc, keys_all, values_all = inner
        key_blk = lax.dynamic_slice_in_dim(shard_piece[0], offset, step_len, 1)
        value_blk = lax.dynamic_slice_in_dim(shard_piece[1], offset, step_len, 1)
        scores = block_scores(query_heads, key_blk, along_rows, along_cols, offset, scale_factor)
        new_max = jnp.maximum(run_max, jnp.max(scores, -1))
        factor = jnp.exp(run_max - new_max)
        weights_blk = jnp.exp(scores - new_max[..., None])
        run_sum = run_sum * factor + jnp.sum(weights_blk, -1)
        value_heads = to_heads(value_blk, heads_local)
        run_acc = run_acc * factor[..., None] + jnp.einsum(
            "ihqk,ihkc->ihqc",
            weights_blk.astype(jnp.bfloat16),
            value_heads,
            preferred_element_type=jnp.float32,
        )
        keys_all = lax.dynamic_update_slice_in_dim(keys_all, key_blk, offset, 1)
        values_all = lax.dynamic_update_slice_in_dim(values_all, value_blk, offset, 1)
        return ((new_max, run_sum, run_acc, keys_all, values_all), None)

    offsets = jnp.arange(piece_len // step_len, dtype=jnp.int32) * step_len
    result, unused = lax.scan(one_step, start_state, offsets)
    run_max, run_sum, run_acc, keys_all, values_all = result
    attn_heads = run_acc / run_sum[..., None]
    log_total = run_max + jnp.log(run_sum)
    attn_low = from_heads(attn_heads).astype(jnp.bfloat16)
    proj_part = jnp.einsum("itd,de->ite", attn_low, proj_full, preferred_element_type=jnp.float32)
    branch = lax.psum_scatter(
        proj_part.astype(jnp.bfloat16), "tp", scatter_dimension=1, tiled=True
    ).astype(jnp.float32)
    middle = resid_in + branch + proj_bias
    normed2 = layer_norm(middle, norm2_gain, norm2_bias).astype(jnp.bfloat16)
    normed2_full = lax.all_gather(normed2, "tp", axis=1, tiled=True)
    hidden_pre = (
        jnp.einsum("itd,df->itf", normed2_full, fc1_full, preferred_element_type=jnp.float32)
        + fc1_local
    )
    gelu_exact = partial(jax.nn.gelu, approximate=False)
    activated_f, gelu_pull = jax.vjp(gelu_exact, hidden_pre)
    activated = activated_f.astype(jnp.bfloat16)
    mlp_part = jnp.einsum("itf,fe->ite", activated, fc2_full, preferred_element_type=jnp.float32)
    mlp_out = lax.psum_scatter(
        mlp_part.astype(jnp.bfloat16), "tp", scatter_dimension=1, tiled=True
    ).astype(jnp.float32)
    output = (middle + mlp_out + fc2_bias).astype(jnp.bfloat16)
    cot_full = lax.all_gather(cotangent, "tp", axis=1, tiled=True)
    d_act = jnp.einsum("ite,fe->itf", cot_full, fc2_full, preferred_element_type=jnp.float32)
    d_hidden = gelu_pull(d_act)[0].astype(jnp.bfloat16)
    fc2_grad = jnp.einsum("itf,ite->fe", activated, cot_full, preferred_element_type=jnp.float32)
    fc1_grad = jnp.einsum("itd,itf->df", normed2_full, d_hidden, preferred_element_type=jnp.float32)
    fc1_bias_part = jnp.sum(d_hidden.astype(jnp.float32), (0, 1))
    fc2_bias_part = jnp.sum(cotangent.astype(jnp.float32), (0, 1))
    d_norm2_part = jnp.einsum("itf,df->itd", d_hidden, fc1_full, preferred_element_type=jnp.float32)
    d_norm2 = lax.psum_scatter(
        d_norm2_part.astype(jnp.bfloat16), "tp", scatter_dimension=1, tiled=True
    ).astype(jnp.float32)
    unused_out, norm2_pull = jax.vjp(layer_norm, middle, norm2_gain, norm2_bias)
    d_mid_part, gain2_part, bias2_part = norm2_pull(d_norm2)
    d_middle = cotangent.astype(jnp.float32) + d_mid_part
    d_branch = d_middle.astype(jnp.bfloat16)
    proj_bias_part = jnp.sum(d_branch.astype(jnp.float32), (0, 1))
    d_branch_full = lax.all_gather(d_branch, "tp", axis=1, tiled=True)
    proj_grad = jnp.einsum(
        "itd,ite->de", attn_low, d_branch_full, preferred_element_type=jnp.float32
    )
    d_attn = jnp.einsum(
        "ite,de->itd", d_branch_full, proj_full, preferred_element_type=jnp.float32
    ).astype(jnp.bfloat16)
    d_attn_heads = to_heads(d_attn, heads_local)
    delta_rows = jnp.sum(d_attn_heads.astype(jnp.float32) * attn_heads, -1)
    key_step = block_size()
    key_rows = key_step // COLS
    key_offsets = jnp.arange(tok_image // key_step, dtype=jnp.int32) * key_step

    def back_step(carried, offset):
        grad_query, grad_rows, grad_cols = carried
        key_blk = lax.dynamic_slice_in_dim(keys_all, offset, key_step, 1)
        value_blk = lax.dynamic_slice_in_dim(values_all, offset, key_step, 1)
        scores = block_scores(query_heads, key_blk, along_rows, along_cols, offset, scale_factor)
        soft_probs = jnp.exp(scores - log_total[..., None])
        value_heads = to_heads(value_blk, heads_local)
        key_heads = to_heads(key_blk, heads_local)
        d_probs = jnp.einsum(
            "ihqc,ihkc->ihqk", d_attn_heads, value_heads, preferred_element_type=jnp.float32
        )
        d_scores = (soft_probs * (d_probs - delta_rows[..., None])).astype(jnp.bfloat16)
        grad_query = grad_query + jnp.einsum(
            "ihqk,ihkc->ihqc", d_scores, key_heads, preferred_element_type=jnp.float32
        )
        grid_scores = d_scores.astype(jnp.float32).reshape(
            images, heads_local, tok_ctx, key_rows, COLS
        )
        row_sums = jnp.sum(grid_scores, 4)
        row_now = lax.dynamic_slice_in_dim(grad_rows, offset // COLS, key_rows, 3)
        grad_rows = lax.dynamic_update_slice_in_dim(
            grad_rows, row_now + row_sums, offset // COLS, 3
        )
        grad_cols = grad_cols + jnp.sum(grid_scores, 3)
        key_part = scale_factor * jnp.einsum(
            "ihqk,ihqc->ikhc", d_scores, query_heads, preferred_element_type=jnp.float32
        )
        value_part = jnp.einsum(
            "ihqk,ihqc->ikhc",
            soft_probs.astype(jnp.bfloat16),
            d_attn_heads,
            preferred_element_type=jnp.float32,
        )
        emitted = (
            key_part.reshape(images, key_step, width_local),
            value_part.reshape(images, key_step, width_local),
        )
        return ((grad_query, grad_rows, grad_cols), emitted)

    back_start = (
        jnp.zeros((images, heads_local, tok_ctx, HD), jnp.float32),
        jnp.zeros((images, heads_local, tok_ctx, grid_rows), jnp.float32),
        jnp.zeros((images, heads_local, tok_ctx, COLS), jnp.float32),
    )
    (grad_query, grad_rows, grad_cols), emitted = lax.scan(back_step, back_start, key_offsets)
    key_terms = emitted[0].transpose(1, 0, 2, 3).reshape(images, tok_image, width_local)
    value_terms = emitted[1].transpose(1, 0, 2, 3).reshape(images, tok_image, width_local)
    grad_keys, grad_values = (
        lax.psum_scatter(
            key_terms.astype(jnp.bfloat16), "ctx", scatter_dimension=1, tiled=True
        ).astype(jnp.float32),
        lax.psum_scatter(
            value_terms.astype(jnp.bfloat16), "ctx", scatter_dimension=1, tiled=True
        ).astype(jnp.float32),
    )
    d_query_rel, rows_grad_part, cols_grad_part = rel_pull((grad_rows, grad_cols))
    d_query = (scale_factor * from_heads(grad_query) + d_query_rel).astype(jnp.bfloat16)
    d_keys = grad_keys.astype(jnp.bfloat16)
    d_values = grad_values.astype(jnp.bfloat16)
    d_projected = jnp.stack((d_query, d_keys, d_values), axis=2)
    qkv_grad = jnp.einsum(
        "itd,itse->sde", normed1_full, d_projected, preferred_element_type=jnp.float32
    )
    qv_bias_part = jnp.stack(
        (
            jnp.sum(d_query.astype(jnp.float32), (0, 1)),
            jnp.sum(d_values.astype(jnp.float32), (0, 1)),
        )
    )
    d_norm1_part = jnp.einsum(
        "itse,sde->itd", d_projected, qkv_full, preferred_element_type=jnp.float32
    )
    d_norm1 = lax.psum_scatter(
        d_norm1_part.astype(jnp.bfloat16), "tp", scatter_dimension=1, tiled=True
    ).astype(jnp.float32)
    unused_in, norm1_pull = jax.vjp(layer_norm, resid_in, norm1_gain, norm1_bias)
    d_in_part, gain1_part, bias1_part = norm1_pull(d_norm1)
    tokens_grad = (d_middle + d_in_part).astype(jnp.bfloat16)
    qkv_out, proj_out, fc1_out, fc2_out = (
        lax.psum_scatter(
            qkv_grad.astype(jnp.bfloat16), ("shard", "ctx"), scatter_dimension=1, tiled=True
        ).astype(jnp.float32),
        lax.psum_scatter(
            proj_grad.astype(jnp.bfloat16), ("shard", "ctx"), scatter_dimension=1, tiled=True
        ).astype(jnp.float32),
        lax.psum_scatter(
            fc1_grad.astype(jnp.bfloat16), ("shard", "ctx"), scatter_dimension=0, tiled=True
        ).astype(jnp.float32),
        lax.psum_scatter(
            fc2_grad.astype(jnp.bfloat16), ("shard", "ctx"), scatter_dimension=1, tiled=True
        ).astype(jnp.float32),
    )
    qv_placed = lax.dynamic_update_slice_in_dim(
        jnp.zeros((2, D), jnp.float32), qv_bias_part, tp_rank * width_local, 1
    )
    fc1_placed = lax.dynamic_update_slice_in_dim(
        jnp.zeros((FF,), jnp.float32), fc1_bias_part, tp_rank * ff_local, 0
    )
    (
        gain1_sum,
        bias1_sum,
        qv_sum,
        rows_sum,
        cols_sum,
        projb_sum,
        gain2_sum,
        bias2_sum,
        fc1b_sum,
        fc2b_sum,
    ) = lax.psum(
        (
            gain1_part,
            bias1_part,
            qv_placed,
            rows_grad_part,
            cols_grad_part,
            proj_bias_part,
            gain2_part,
            bias2_part,
            fc1_placed,
            fc2_bias_part,
        ),
        ("shard", "ctx", "tp"),
    )
    return (
        output,
        tokens_grad,
        gain1_sum,
        bias1_sum,
        qkv_out,
        qv_sum,
        rows_sum,
        cols_sum,
        proj_out,
        projb_sum,
        gain2_sum,
        bias2_sum,
        fc1_out,
        fc1b_sum,
        fc2_out,
        fc2b_sum,
    )


F32 = jnp.float32
BF16 = jnp.bfloat16
NT = (((1,), (1,)), ((), ()))
NN = (((1,), (0,)), ((), ()))
TN = (((0,), (0,)), ((), ()))
VMEM_GRANT = 60 * 2**20
DMA = pltpu.SemaphoreType.DMA
ANY = pl.BlockSpec(memory_space=pl.ANY)
VM = pl.BlockSpec(memory_space=pltpu.VMEM)


def mm(left, right, dims=NN):
    return lax.dot_general(left, right, dims, preferred_element_type=F32)


def lane_ids(shape):
    return lax.broadcasted_iota(jnp.int32, shape, 1)


def place():
    return lax.axis_index("shard"), lax.axis_index("ctx"), lax.axis_index("tp")


def core_mate(t):
    return t + 1 - 2 * lax.rem(t, 2)


def far_mate(t):
    return lax.rem(t + 2, 4)


def aim(src, dst, sems, k, where):
    return pltpu.make_async_remote_copy(
        src_ref=src,
        dst_ref=dst,
        send_sem=sems.at[0, k],
        recv_sem=sems.at[1, k],
        device_id=where,
        device_id_type=pl.DeviceIdType.MESH,
    )


def send(src, dst, sems, k, where):
    copy = aim(src, dst, sems, k, where)
    copy.start()
    return copy


def swap_copy(src, dst, sems):
    _, c, _ = place()
    return pltpu.make_async_remote_copy(
        src_ref=src,
        dst_ref=dst,
        send_sem=sems.at[0, 0],
        recv_sem=sems.at[1, 0],
        device_id={"ctx": 1 - c},
        device_id_type=pl.DeviceIdType.MESH,
    )


def fill_tables(tab_ref, rr_ref, rc_ref):
    tab_ref[...] = jnp.zeros_like(tab_ref)
    tab_ref[0 : rr_ref.shape[0], 0 : rr_ref.shape[1]] = rr_ref[...]
    tab_ref[128 : 128 + rc_ref.shape[0], 0 : rc_ref.shape[1]] = rc_ref[...]


def fill_hots(hot_ref, hd, cols, rows, second):
    shift = cols.bit_length() - 1
    down = lax.broadcasted_iota(jnp.int32, hot_ref.shape, 0)
    kr = lax.shift_right_logical(down, shift)
    kw = down & (cols - 1)
    l = lane_ids(hot_ref.shape)
    if second:
        hit = (l == hd + rows - 1 - kr) | (l == 128 + cols - 1 - kw)
    else:
        hit = (l == hd + kr) | (l == hd + rows + kr) | (l == 128 + kw) | (l == 192 + kw)
    hot_ref[...] = jnp.where(hit, 1.0, 0.0).astype(BF16)


def reverser(top):
    down = lax.broadcasted_iota(jnp.int32, (128, 128), 0)
    return jnp.where(down + lane_ids((128, 128)) == top, 1.0, 0.0).astype(BF16)


def greet(shards, line=False):
    s, c, t = place()
    size = 2 * shards
    at = s * (1 - c) + (size - 1 - s) * c
    peers = [{"ctx": 1 - c}, {"tp": core_mate(t)}, {"tp": far_mate(t)}]
    for step in (1, size - 1):
        to = lax.rem(at + step, size)
        back = to // shards
        peers.append({"shard": to * (1 - back) + (size - 1 - to) * back, "ctx": back})
    if line:
        peers += [{"shard": lax.rem(s + d, shards)} for d in range(1, shards)]
    barrier = pltpu.get_barrier_semaphore()
    for peer in peers:
        pl.semaphore_signal(barrier, inc=1, device_id=peer, device_id_type=pl.DeviceIdType.MESH)
    pl.semaphore_wait(barrier, len(peers))


class Ring:
    def __init__(self, shards, block, sems):
        s, c, _ = place()
        self.shards, self.size, self.sems = shards, 2 * shards, sems
        self.at = s * (1 - c) + (self.size - 1 - s) * c
        self.half = block // 2
        self.pieces = ring_pieces(block)
        self.rows = self.half // self.pieces
        self.first, self.end = self.pieces, self.pieces * (self.size - 1)
        self.now = self.first

    def coords(self, position):
        back = position // self.shards
        return position * (1 - back) + (self.size - 1 - position) * back, back

    def peer(self, way):
        to = lax.rem(self.at + (1 if way == 0 else self.size - 1), self.size)
        shard, ctx = self.coords(to)
        return {"shard": shard, "ctx": ctx}

    def owner(self, offset):
        shard, ctx = self.coords(lax.rem(self.at + 2 * self.size + offset, self.size))
        return 2 * shard + ctx

    def split(self, event):
        if isinstance(event, int):
            return event // self.pieces, event % self.pieces
        return lax.div(event, self.pieces), lax.rem(event, self.pieces)

    def rows_of(self, way, piece):
        start = way * self.half + piece * self.rows
        return pl.ds(start if isinstance(start, int) else pl.multiple_of(start, self.rows), self.rows)

    def make(self, src, dst, way, event):
        slot = way * self.end + event
        return pltpu.make_async_remote_copy(
            src_ref=src,
            dst_ref=dst,
            send_sem=self.sems.at[0, slot],
            recv_sem=self.sems.at[1, slot],
            device_id=self.peer(way),
            device_id_type=pl.DeviceIdType.MESH,
        )

    def run(self, low, high):
        low, high = max(low, self.first), min(high, self.end)
        if low < high:
            lax.fori_loop(low, high, lambda event, _: (self.step(event), 0)[1], 0)

    def tick(self, count):
        self.run(self.now, self.now + count)
        self.now += count

    def poll(self, event):
        pl.when((event >= self.first) & (event < self.end))(lambda: self.step(event))


def ring_pieces(block):
    return 5 if block % 160 == 0 else 1


def ring_sems(shards, block):
    return DMA((2, 2 * ring_pieces(block) * (2 * shards - 1)))


class Spread(Ring):
    def __init__(self, shards, src, dst, sems, local):
        super().__init__(shards, src.shape[0], sems)
        self.src, self.dst = src, dst
        self.local = pltpu.make_async_copy(src, dst.at[self.owner(0)], local)
        self.local.start()
        for event in range(self.first):
            for way in range(2):
                self.hop(way, event, True).start()

    def hop(self, way, event, own=False):
        j, piece = self.split(event)
        rows = self.rows_of(way, piece)
        there = self.dst.at[self.owner(-j if way == 0 else j), rows]
        return self.make(self.src.at[rows] if own else there, there, way, event)

    def step(self, event):
        for way in range(2):
            self.hop(way, event - self.pieces).wait_recv()
            self.hop(way, event).start()

    def finish(self):
        self.local.wait()
        for way in range(2):
            for event in range(self.end - self.pieces, self.end):
                self.hop(way, event).wait_recv()

        def sent(event, _):
            for way in range(2):
                self.hop(way, event).wait_send()
            return 0

        lax.fori_loop(0, self.end, sent, 0)

    @staticmethod
    def scratch(shards, block):
        return [ring_sems(shards, block[0]), DMA]


class Collect(Ring):
    def __init__(self, shards, src, held, sems):
        super().__init__(shards, src.shape[0] // (2 * shards), sems)
        self.src, self.held, self.block = src, held, src.shape[0] // (2 * shards)

    def begin(self):
        for event in range(self.first):
            for way in range(2):
                self.hop(way, event, True).start()

    def pair_rows(self, n, j):
        offset = (n + 1) * (2 * j - 1)
        last = (2 * n + j + 1) // self.size
        return pl.ds(pl.multiple_of(self.owner(offset * (1 - last)) * self.block, self.rows), self.block)

    def own(self, way, j, piece):
        ahead = self.size - 1 - j
        start = self.owner(ahead if way == 0 else -ahead) * self.block + way * self.half + piece * self.rows
        return pl.ds(pl.multiple_of(start, self.rows), self.rows)

    def hop(self, way, event, own=False):
        j, piece = self.split(event)
        rows = self.rows_of(0, piece)
        there = self.held.at[way, j, rows]
        here = self.src.at[self.own(way, j, piece)] if own else self.held.at[way, j - 1, rows]
        return self.make(here, there, way, event)

    def arrived(self, way, event):
        j, piece = self.split(event)
        there = self.held.at[way, j, self.rows_of(0, piece)]
        self.make(there, there, way, event).wait_recv()

    def step(self, event):
        j, piece = self.split(event)
        rows = self.rows_of(0, piece)
        for way in range(2):
            self.arrived(way, event - self.pieces)
            both = self.held[way, j - 1, rows].astype(F32) + self.src[self.own(way, j, piece)].astype(F32)
            self.held[way, j - 1, rows] = both.astype(BF16)
            self.hop(way, event).start()

    def finish(self, out):
        for piece in range(self.pieces):
            for way in range(2):
                self.arrived(way, self.end - self.pieces + piece)
                last = self.held[way, self.size - 2, self.rows_of(0, piece)].astype(F32)
                own = self.src[self.own(way, self.size - 1, piece)].astype(F32)
                out[self.rows_of(way, piece)] = last + own

        def sent(event, _):
            for way in range(2):
                j, piece = self.split(event)
                there = self.held.at[way, j, self.rows_of(0, piece)]
                self.make(there, there, way, event).wait_send()
            return 0

        lax.fori_loop(0, self.end, sent, 0)

    @staticmethod
    def scratch(shards, block):
        return [pltpu.VMEM((2, 2 * shards - 1, block[0] // 2, block[1]), BF16), ring_sems(shards, block[0])]


class Share:
    def __init__(self, full, sems):
        self.full, self.sems = full, sems

    def copies(self, k, p, src=None):
        _, _, t = place()
        block, passed = self.full.at[p, t], self.full.at[p, far_mate(t)]
        src = block if src is None else src
        return (
            partial(aim, src, block, self.sems, 3 * k, {"tp": far_mate(t)}),
            partial(aim, src, block, self.sems, 3 * k + 1, {"tp": core_mate(t)}),
            partial(aim, passed, passed, self.sems, 3 * k + 2, {"tp": core_mate(t)}),
        )

    def push(self, k, p, src=None):
        for copy in self.copies(k, p, src)[:2]:
            copy().start()

    def forward(self, k, p):
        far, _, third = self.copies(k, p)
        far().wait_recv()
        third().start()

    def finish(self, k, p):
        far, core, third = self.copies(k, p)
        far().wait_send()
        core().wait()
        third().wait()


class Gather2:
    def __init__(self, part, mate, far, out, sems):
        self.part, self.mate, self.far, self.out, self.sems = part, mate, far, out, sems

    def copies(self, p):
        _, _, t = place()
        m = core_mate(t)
        return (
            partial(aim, self.part.at[p, far_mate(m)], self.mate.at[p, 1], self.sems, 3 * p, {"tp": m}),
            partial(aim, self.part.at[p, m], self.mate.at[p, 0], self.sems, 3 * p + 1, {"tp": m}),
            partial(aim, self.out.at[p], self.far.at[p], self.sems, 3 * p + 2, {"tp": far_mate(t)}),
        )

    def push(self, p):
        for copy in self.copies(p)[:2]:
            copy().start()

    def forward(self, p):
        _, _, t = place()
        passing, _, onward = self.copies(p)
        passing().wait_recv()
        both = self.part[p, far_mate(t)].astype(F32) + self.mate[p, 1].astype(F32)
        self.out[p] = both.astype(BF16)
        onward().start()

    def result(self, p):
        _, _, t = place()
        _, own, onward = self.copies(p)
        own().wait_recv()
        onward().wait_recv()
        return self.part[p, t].astype(F32) + self.mate[p, 0].astype(F32) + self.far[p].astype(F32)

    def finish(self, p):
        for copy in self.copies(p):
            copy().wait_send()

    @staticmethod
    def scratch(block):
        return [
            pltpu.VMEM((2, 2) + block, BF16),
            pltpu.VMEM((2,) + block, BF16),
            pltpu.VMEM((2,) + block, BF16),
            DMA((2, 6)),
        ]


def ln_stats(values):
    average = jnp.mean(values, -1, keepdims=True)
    centred = values - average
    inverse = lax.rsqrt(jnp.mean(centred * centred, -1, keepdims=True) + EPSILON)
    return centred * inverse, inverse


def ln_back(unit, inverse, gain, grad):
    scaled = grad * gain
    first = jnp.mean(scaled, -1, keepdims=True)
    second = jnp.mean(scaled * unit, -1, keepdims=True)
    return inverse * (scaled - first - unit * second)


def row_tiles(out_ref, left_ref, right_ref, dims, first, count, tile=256):
    def one(i, _):
        at = pl.ds(pl.multiple_of(i * tile, tile), tile)
        out_ref[at, :] = mm(left_ref[at, :], right_ref[...], dims).astype(out_ref.dtype)
        return 0

    lax.fori_loop(first, first + count, one, 0)


def grad_tiles(out_ref, left_ref, right_ref, first, count, cols=slice(None), tile=256):
    def one(i, _):
        at = pl.ds(pl.multiple_of(i * tile, tile), tile)
        out_ref[at, cols] = mm(left_ref[:, at], right_ref[...], TN).astype(out_ref.dtype)
        return 0

    lax.fori_loop(first, first + count, one, 0)


def comm_call(kernel, name, ident, args, outs, scratch, hbm_in=(), hbm_out=()):
    return pl.pallas_call(
        kernel,
        out_shape=tuple(outs),
        in_specs=[ANY if i in hbm_in else VM for i in range(len(args))],
        out_specs=tuple(ANY if i in hbm_out else VM for i in range(len(outs))),
        scratch_shapes=scratch,
        compiler_params=pltpu.CompilerParams(
            vmem_limit_bytes=VMEM_GRANT, collective_id=ident, has_side_effects=True
        ),
        name=name,
    )(*args)


def turned(out_ref, full_ref, p):
    count, length = full_ref.shape[1:3]

    def one(i, _):
        start = pl.multiple_of((p * count + i) * length, 128)
        out_ref[:, pl.ds(start, length)] = full_ref[p, i].T
        return 0

    lax.fori_loop(0, count, one, 0)


def front_kernel(
    shards, tok_ref, qkvw_ref, pw_ref, vec_ref, x_ref, a_ref, wf_ref, at_ref,
    w1_ref, swap_sems, share_sems, w_sems, w_local,
):
    s, c, t = place()
    wide = qkvw_ref.shape[2]
    for j in range(3):
        w1_ref[:, j * wide : (j + 1) * wide] = qkvw_ref[j]
    w1_ref[:, 3 * wide : 4 * wide] = pw_ref[...]
    greet(shards)
    swap = send(tok_ref.at[1 - c], x_ref.at[c], swap_sems, 0, {"ctx": 1 - c})
    spread = Spread(shards, w1_ref, wf_ref, w_sems, w_local)
    share = Share(a_ref, share_sems)

    def norm(block):
        unit, _ = ln_stats(block.astype(F32))
        return (unit * vec_ref[0:1, :] + vec_ref[1:2, :]).astype(BF16)

    own = tok_ref[c]
    x_ref[c] = own
    a_ref[c, t] = norm(own)
    share.push(0, c)
    swap.wait()
    a_ref[1 - c, t] = norm(x_ref[1 - c])
    share.push(1, 1 - c)
    share.forward(0, c)
    spread.tick(9)
    share.forward(1, 1 - c)
    spread.tick(6)
    share.finish(0, c)
    share.finish(1, 1 - c)
    turned(at_ref, a_ref, 0)
    spread.tick(2)
    spread.tick(4)
    turned(at_ref, a_ref, 1)
    spread.tick(2)
    spread.tick(spread.end)
    spread.finish()


def fwd_kernel(
    shards, heads, hd, cols, rows, qb,
    a1_ref, w1_ref, vec_ref, rr_ref, rc_ref, cot_ref, w_ref,
    vh_ref, oh_ref, ob_ref, lse_ref, qa_ref, ka_ref, g_ref, cf_ref, wf_ref, pp_ref,
    qh_ref, vt_ref, rt_ref, tab_ref, hot_ref, swap_sems, share_sems, w_sems, w_local,
):
    _, me, t = place()
    tok, width = ob_ref.shape
    wide = 3 * width
    blocks = tok // qb
    fill_tables(tab_ref, rr_ref, rc_ref)
    fill_hots(hot_ref, hd, cols, rows, False)
    rt_ref[0:128, :] = mm(reverser(2 * rows - 2), tab_ref[0:128, :]).astype(BF16)
    rt_ref[128:256, :] = mm(reverser(2 * cols - 2), tab_ref[128:256, :]).astype(BF16)
    greet(shards)
    swap = swap_copy(cot_ref.at[1 - me], g_ref.at[me], swap_sems)
    swap.start()
    spread = Spread(shards, w_ref, wf_ref, w_sems, w_local)
    share = Share(cf_ref, share_sems)
    own = cot_ref[me]
    g_ref[me] = own
    cf_ref[me, t] = own
    share.push(0, me, cot_ref.at[me])

    def project(i, _):
        at = pl.ds(pl.multiple_of(i * qb, qb), qb)
        tile = (mm(a1_ref[at, :], w1_ref[:, 0:wide]) + vec_ref[7:8, 0:wide]).astype(BF16)
        pad = jnp.zeros((qb, 128 - hd), BF16)
        front = lane_ids((qb, 128)) < hd
        for h in range(heads):
            part = [tile[:, (j * heads + h) * hd : (j * heads + h + 1) * hd] for j in range(3)]
            part = [jnp.concatenate([x, pad], 1) for x in part]
            qh_ref[h, at, :] = part[0]
            ka_ref[h, at, 0:128] = jnp.where(front, part[1], hot_ref[at, 0:128])
            ka_ref[h, at, 128:256] = hot_ref[at, 128:256]
            vh_ref[h, at, :] = part[2]
        return 0

    lax.fori_loop(0, blocks, project, 0)
    swap.wait()
    cf_ref[1 - me, t] = g_ref[1 - me]
    share.push(1, 1 - me, g_ref.at[1 - me])
    c = hd**-0.5 * math.log2(math.e)
    up = hd**0.5

    def head(h, _):
        vt_ref[...] = vh_ref[h].T
        terms = mm(qh_ref[h], rt_ref[...], NT) * up
        ln = lane_ids((cols, 128))
        for r in range(rows):
            rs = slice(r * cols, (r + 1) * cols)
            tr = pltpu.roll(terms[rs, 0:128], (65 + r) % 128, 1)
            tc = pltpu.roll(terms[rs, 128:256], 65, 1, stride=1, stride_axis=0)
            rh = tr.astype(BF16).astype(F32)
            rl = pltpu.roll(tr - rh, rows, 1)
            ch = tc.astype(BF16).astype(F32)
            cl = pltpu.roll(tc - ch, 64, 1)
            low = jnp.where(ln < hd + 2 * rows, rl, jnp.zeros_like(tr))
            left = jnp.where(ln < hd, qh_ref[h, rs, :].astype(F32), jnp.where(ln < hd + rows, rh, low))
            qa_ref[h, rs, 0:128] = left.astype(BF16)
            qa_ref[h, rs, 128:256] = jnp.where(ln < 64, ch, cl).astype(BF16)

        def blk(i, _):
            at = pl.ds(pl.multiple_of(i * qb, qb), qb)
            s = mm(ka_ref[h], qa_ref[h, at, :], NT)
            m = jnp.max(s, 0, keepdims=True)
            p = jnp.exp2((s - m) * c)
            l = jnp.sum(p, 0, keepdims=True)
            lse_ref[h, :, at] = m * c + jnp.log2(l)
            oh_ref[h, at, :] = (mm(vt_ref[...], p.astype(BF16)) / l).T
            for k in range(2):
                spread.poll(spread.first + 2 * (h * blocks + i) + k)
            return 0

        lax.fori_loop(0, blocks, blk, 0)
        pl.when(h == 0)(lambda: share.forward(0, me))
        pl.when(h == min(1, heads - 1))(lambda: share.forward(1, 1 - me))
        return 0

    lax.fori_loop(0, heads, head, 0)
    for h in range(heads):
        ob_ref[:, h * hd : (h + 1) * hd] = oh_ref[h, :, 0:hd].astype(BF16)

    def out_rows(i, _):
        at = pl.ds(pl.multiple_of(i * qb, qb), qb)
        pp_ref[at, :] = mm(ob_ref[at, :], w1_ref[:, wide:], NT).astype(BF16)
        return 0

    lax.fori_loop(0, blocks, out_rows, 0)
    spread.run(spread.first + 2 * heads * blocks, spread.end)
    share.finish(0, me)
    share.finish(1, 1 - me)
    spread.finish()


def mid_kernel(
    shards, part_ref, x_ref, vec_ref, w_ref, f1_ref, cf_ref,
    mid_ref, a_ref, wf_ref, act_ref, slope_ref, ct_ref,
    mate, far, outb, sum_sems, share_sems, w_sems, w_local,
):
    _, _, t = place()
    greet(shards)
    gather = Gather2(part_ref, mate, far, outb, sum_sems)
    gather.push(0)
    gather.push(1)
    spread = Spread(shards, w_ref, wf_ref, w_sems, w_local)
    share = Share(a_ref, share_sems)
    gather.forward(0)
    gather.forward(1)
    turned(ct_ref, cf_ref, 0)
    spread.tick(8)
    for p in range(2):
        mid = x_ref[p].astype(F32) + gather.result(p) + vec_ref[2:3, :]
        mid_ref[p] = mid
        unit, _ = ln_stats(mid)
        a_ref[p, t] = (unit * vec_ref[3:4, :] + vec_ref[4:5, :]).astype(BF16)
        share.push(p, p)
        if p == 1:
            turned(ct_ref, cf_ref, 1)
        spread.tick(7)
    share.forward(0, 0)
    half = a_ref.shape[1] * a_ref.shape[2]

    def hidden(p):
        def one(i, _):
            rows = a_ref[p, pl.ds(2 * i, 2)].reshape(-1, a_ref.shape[3])
            pre = mm(rows, f1_ref[...]) + vec_ref[6:7, :]
            cdf = 0.5 * (1.0 + lax.erf(pre * (2.0**-0.5)))
            bell = jnp.exp(-0.5 * pre * pre) * ((2.0 * math.pi) ** -0.5)
            at = pl.ds(pl.multiple_of(p * half + i * rows.shape[0], 128), rows.shape[0])
            act_ref[at, :] = (pre * cdf).astype(BF16)
            slope_ref[at, :] = cdf + pre * bell
            for k in range(2):
                spread.poll(base + 2 * i + k)
            return 0

        base = spread.now
        lax.fori_loop(0, a_ref.shape[1] // 2, one, 0)
        spread.now += a_ref.shape[1]

    share.finish(0, 0)
    hidden(0)
    spread.tick(spread.end)
    share.forward(1, 1)
    share.finish(1, 1)
    hidden(1)
    for p in range(2):
        gather.finish(p)
    spread.finish()


def turn_kernel(
    shards, ct_ref, act_ref, slope_ref, cot_ref, f2_ref, f1_ref, a2_ref, mid_ref, g_ref, vec_ref, w1_ref,
    dm_ref, db_ref, dbt_ref, wg_ref, sums_ref, f1g_ref, mlp_ref, do_ref,
    w2g_ref, part_ref, dp_ref, mate, far, outb, sum_sems, share_sems, w_held, w_sems,
):
    _, _, t = place()
    greet(shards)
    collect = Collect(shards, w2g_ref, w_held, w_sems)
    gather = Gather2(part_ref, mate, far, outb, sum_sems)
    share = Share(db_ref, share_sems)
    tile = 2 * db_ref.shape[2]
    halves = db_ref.shape[1] // 2
    sums_ref[...] = jnp.zeros_like(sums_ref)
    step = collect.pieces

    def back(n, _):
        def block(j, _):
            at = collect.pair_rows(n, j)
            w2g_ref[at, :] = mm(ct_ref[at, :], act_ref[...]).astype(BF16)
            return 0

        lax.fori_loop(0, 2, block, 0)
        pl.when(n == 0)(collect.begin)
        pl.when(n == halves)(lambda: gather.forward(0))
        p, i = n // halves, n % halves
        at = pl.ds(pl.multiple_of(n * tile, tile), tile)
        d_pre = (mm(cot_ref[at, :], f2_ref[...]) * slope_ref[at, :]).astype(BF16)
        dp_ref[at, :] = d_pre
        sums_ref[4:5, :] += jnp.sum(d_pre.astype(F32), 0, keepdims=True)
        for k in range(2):
            collect.poll(step * n + k)
        d_a2 = mm(d_pre, f1_ref[...], NT).astype(BF16)
        part_ref[p, pl.ds(2 * i, 2)] = d_a2.reshape(2, tile // 2, -1)
        pl.when(n == halves - 1)(lambda: gather.push(0))
        for k in range(2, step):
            collect.poll(step * n + k)
        return 0

    lax.fori_loop(0, 2 * halves, back, 0)
    gather.push(1)
    base = 2 * halves * step

    def hidden_grad(i, _):
        at = pl.ds(pl.multiple_of(i * 256, 256), 256)
        f1g_ref[at, :] = mm(a2_ref[:, at], dp_ref[...], TN).astype(BF16)
        collect.poll(base + i)
        pl.when(i == 0)(lambda: gather.forward(1))

        @pl.when((i == 1) | (i == count - 1))
        def _():
            p = lax.div(i, count - 1)
            unit, inverse = ln_stats(mid_ref[p])
            g = g_ref[p].astype(F32)
            da = gather.result(p)
            dm = g + ln_back(unit, inverse, vec_ref[3:4, :], da)
            dm_ref[p] = dm
            low_dm = dm.astype(BF16)
            db_ref[p, t] = low_dm
            share.push(p, p)
            for k, term in enumerate((da * unit, da, low_dm.astype(F32), g)):
                sums_ref[k : k + 1, :] += jnp.sum(term, 0, keepdims=True)

        return 0

    count = f1g_ref.shape[0] // 256
    lax.fori_loop(0, count, hidden_grad, 0)
    base2 = base + count

    def mlp(n, _):
        at = pl.ds(pl.multiple_of(n * tile, tile), tile)
        mlp_ref[at, :] = mm(act_ref[at, :], f2_ref[...], NT).astype(BF16)
        for k in range(2):
            collect.poll(base2 + 2 * n + k)
        pl.when(n == 2 * halves - 1)(lambda: share.forward(0, 0))
        return 0

    lax.fori_loop(0, 2 * halves, mlp, 0)
    collect.run(base2 + 4 * halves, collect.end)
    share.forward(1, 1)
    wide = do_ref.shape[1]

    def d_o(n, _):
        p, i = n // halves, n % halves
        pl.when(i == 0)(lambda: share.finish(p, p))
        rows = db_ref[p, pl.ds(2 * i, 2)].reshape(tile, -1)
        at = pl.ds(pl.multiple_of(n * tile, tile), tile)
        do_ref[at, :] = mm(rows, w1_ref[:, 3 * wide :]).astype(BF16)
        dbt_ref[:, at] = rows.T
        return 0

    lax.fori_loop(0, 2 * halves, d_o, 0)
    for p in range(2):
        gather.finish(p)
    collect.finish(wg_ref)


def bwd_kernel(
    shards, heads, hd, cols, rows, qb,
    qa_ref, ka_ref, vh_ref, do_ref, oh_ref, lse_ref, rr_ref, rc_ref, w_ref, part_ref, mid_ref, vec_ref,
    dqkv_ref, rg_ref, wg_ref, qs_ref, out_ref,
    doh_ref, dh_ref, kt_ref, acc_k, acc_v, del_ref, tab_ref, hot_ref, res_ref,
    mate, far, outb, sum_sems, swap_sems, w_held, w_sems,
):
    fill_tables(tab_ref, rr_ref, rc_ref)
    fill_hots(hot_ref, hd, cols, rows, True)
    _, me, _ = place()
    greet(shards)
    gather = Gather2(part_ref, mate, far, outb, sum_sems)
    gather.push(0)
    gather.push(1)
    swap = swap_copy(res_ref.at[1 - me], out_ref.at[me], swap_sems)
    collect = Collect(shards, w_ref, w_held, w_sems)
    collect.begin()
    tok, wide = dqkv_ref.shape
    blocks = tok // qb
    for h in range(heads):
        pad = jnp.zeros((tok, 128 - hd), BF16)
        doh_ref[h] = jnp.concatenate([do_ref[:, h * hd : (h + 1) * hd], pad], 1)
    gather.forward(0)
    gather.forward(1)
    scale = hd**-0.5
    c = scale * math.log2(math.e)
    rg_ref[...] = jnp.zeros_like(rg_ref)

    def head(h, _):
        kt_ref[0:128, :] = jnp.where(lane_ids((tok, 128)) < hd, ka_ref[h, :, 0:128], hot_ref[:, 0:128]).T
        kt_ref[128:256, :] = hot_ref[:, 128:256].T
        del_ref[...] = lax.dot_general(
            jnp.ones((8, 128), F32), doh_ref[h].astype(F32) * oh_ref[h], NT,
            preferred_element_type=F32, precision=PRECISE,
        )
        acc_k[...] = jnp.zeros_like(acc_k)
        acc_v[...] = jnp.zeros_like(acc_v)

        def blk(i, _):
            at = pl.ds(pl.multiple_of(i * qb, qb), qb)
            qblk = qa_ref[h, at, :]
            dob = doh_ref[h, at, :]
            s = mm(ka_ref[h], qblk, NT)
            p = jnp.exp2(s * c - lse_ref[h, :, at])
            dp = mm(vh_ref[h], dob, NT)
            ds = (p * (dp - del_ref[0:1, at])).astype(BF16)
            acc_v[...] += mm(p.astype(BF16), dob)
            acc_k[...] += mm(ds, qblk[:, 0:128])
            dqa = mm(kt_ref[...], ds).T
            ln = lane_ids((cols, 128))
            parts = []
            for j in range(qb // cols):
                r = i * (qb // cols) + j
                js = slice(j * cols, (j + 1) * cols)
                dr = dqa[js, 0:128]
                dr = jnp.where((ln >= hd) & (ln < hd + rows), dr, 0.0)
                dr = pltpu.roll(dr, lax.rem(48 + r, 128), 1)
                dc = pltpu.roll(dqa[js, 128:256], 0, 1, stride=1, stride_axis=0)
                parts.append(jnp.concatenate([dr, dc], 1))
            d = jnp.concatenate(parts, 0).astype(BF16)
            rel = mm(d, tab_ref[...])
            rg_ref[...] += mm(d, qblk[:, 0:128], TN)
            dh_ref[h, at, :] = (scale * dqa[:, 0:128] + rel).astype(BF16)
            for k in range(2):
                collect.poll(collect.first + 2 * (h * blocks + i) + k)
            return 0

        lax.fori_loop(0, blocks, blk, 0)
        dh_ref[heads + h] = (scale * acc_k[...]).astype(BF16)
        dh_ref[2 * heads + h] = acc_v[...].astype(BF16)

        @pl.when(h == min(2, heads - 1))
        def _():
            for p in range(2):
                total = mid_ref[p] + gather.result(p) + vec_ref[5:6, :]
                res_ref[p] = total.astype(BF16)

        return 0

    lax.fori_loop(0, heads, head, 0)
    swap.start()
    out_ref[me] = res_ref[me]
    for j in range(3 * heads):
        dqkv_ref[:, j * hd : (j + 1) * hd] = dh_ref[j, :, 0:hd]
    collect.run(collect.first + 2 * heads * blocks, collect.end)
    qs_ref[...] = mm(jnp.ones((8, tok), BF16), dqkv_ref[...])
    for p in range(2):
        gather.finish(p)
    collect.finish(wg_ref)
    swap.wait()


def end_kernel(
    shards, x_ref, dm_ref, vec_ref, at_ref, dqkv_ref, dbt_ref, ob_ref, small_ref, w1_ref,
    grad_ref, qg_ref, pg_ref, total_ref,
    w1g_ref, wg_ref, part_ref, gres_ref, mate, far, outb, sum_sems, swap_sems,
    held, got, line, small_sems, w_held, w_sems,
):
    s, me, t = place()
    greet(shards, True)
    gather = Gather2(part_ref, mate, far, outb, sum_sems)
    collect = Collect(shards, w1g_ref, w_held, w_sems)
    wide = dqkv_ref.shape[1]
    tile = 2 * part_ref.shape[2]
    halves = part_ref.shape[1] // 2
    step = collect.pieces

    def back(n, _):
        p, i = n // halves, n % halves
        rows = pl.ds(pl.multiple_of(n * tile, tile), tile)
        d_a1 = mm(dqkv_ref[rows, :], w1_ref[:, 0:wide], NT).astype(BF16)
        part_ref[p, pl.ds(2 * i, 2)] = d_a1.reshape(2, tile // 2, -1)
        pl.when(n == halves - 1)(lambda: gather.push(0))
        for k in range(step):
            collect.poll(step * (n - 1) + k)

        def block(j, _):
            at = collect.pair_rows(n, j)
            w1g_ref[at, 0:wide] = mm(at_ref[at, :], dqkv_ref[...]).astype(BF16)
            w1g_ref[at, wide:] = mm(dbt_ref[at, :], ob_ref[...]).astype(BF16)
            return 0

        lax.fori_loop(0, 2, block, 0)
        pl.when(n == 0)(collect.begin)
        pl.when(n == halves)(lambda: gather.forward(0))
        return 0

    lax.fori_loop(0, 2 * halves, back, 0)
    gather.push(1)
    collect.now = step * (2 * halves - 1)
    collect.tick(2)
    gather.forward(1)
    collect.tick(2)
    held[0] = small_ref[...]
    for p in range(2):
        unit, inverse = ln_stats(x_ref[p].astype(F32))
        collect.tick(2)
        da = gather.result(p)
        gres_ref[p] = (dm_ref[p] + ln_back(unit, inverse, vec_ref[0:1, :], da)).astype(BF16)
        held[0, 0:1, :] += jnp.sum(da * unit, 0, keepdims=True)
        held[0, 1:2, :] += jnp.sum(da, 0, keepdims=True)
        collect.tick(3)
    grad_ref[me] = gres_ref[me]
    swap = swap_copy(gres_ref.at[1 - me], grad_ref.at[me], swap_sems)
    waits = []
    for k, peer in enumerate(({"tp": core_mate(t)}, {"tp": far_mate(t)}, {"ctx": 1 - me})):
        copy = send(held.at[k], got.at[k], small_sems, k, peer)
        if k == 2:
            swap.start()
        collect.tick(2)
        copy.wait_recv()
        waits.append(copy)
        held[k + 1] = held[k] + got[k]
    line[s] = held[3]
    for d in range(1, shards):
        waits.append(send(held.at[3], line.at[s], small_sems, 2 + d, {"shard": lax.rem(s + d, shards)}))
    collect.tick(collect.end)
    collect.finish(wg_ref)
    part = wide // 3
    for j in range(3):
        qg_ref[j] = wg_ref[:, j * part : (j + 1) * part]
    pg_ref[...] = wg_ref[:, wide:]
    for k, copy in enumerate(waits):
        if k < 3:
            copy.wait_send()
        else:
            copy.wait()
    acc = line[0]
    for k in range(1, shards):
        acc = acc + line[k]
    total_ref[...] = acc
    for p in range(2):
        gather.finish(p)
    swap.wait()


def on_device_images(
    tokens, norm1_gain, norm1_bias, qkv_weight, qv_bias, rel_rows, rel_cols, proj_weight, proj_bias,
    norm2_gain, norm2_bias, fc1_weight, fc1_bias, fc2_weight, fc2_bias, cotangent,
):
    S = jax.ShapeDtypeStruct
    shards = lax.axis_size("shard")
    tp_count = lax.axis_size("tp")
    tp_rank = lax.axis_index("tp")
    heads = H // tp_count
    width = heads * HD
    ff = FF // tp_count
    rows = (rel_rows.shape[0] + 1) // 2
    tok = rows * COLS
    own = tokens.shape
    piece = own[1:]
    full = (2, tp_count) + piece
    block = fc1_weight.shape
    blocks = (2 * shards,) + block
    qkv_cols = 3 * width
    fc2_t = fc2_weight.T
    qv_local = lax.dynamic_slice_in_dim(qv_bias, tp_rank * width, width, 1)
    qkv_bias = jnp.concatenate([qv_local[0], jnp.zeros((width,), F32), qv_local[1]])
    fc1_local = lax.dynamic_slice_in_dim(fc1_bias, tp_rank * ff, ff, 0)
    vec = jnp.concatenate(
        [
            norm1_gain, norm1_bias, proj_bias, norm2_gain, norm2_bias, fc2_bias, fc1_local,
            qkv_bias, jnp.zeros((D - qkv_cols,), F32),
        ]
    ).reshape(8, D)
    spread = Spread.scratch(shards, block)
    collect = Collect.scratch(shards, block)
    gather = Gather2.scratch(piece)
    swap = [DMA((2, 1))]
    share = [DMA((2, 6))]

    x, a1, w1_full, a1_turned = comm_call(
        partial(front_kernel, shards), "front", 0,
        (tokens, qkv_weight, proj_weight.T, vec),
        (S(own, BF16), S(full, BF16), S(blocks, BF16), S((D, tok), BF16)),
        [pltpu.VMEM(block, BF16)] + swap + share + spread, hbm_out=(2,),
    )
    w1_full = w1_full.reshape(D, -1)
    vh, oh, o_low, lse, qa, ka, g, cot, fc1_full, proj_part = comm_call(
        partial(fwd_kernel, shards, heads, HD, COLS, rows, 256), "attn_fwd", 1,
        (a1.reshape(tok, D), w1_full, vec, rel_rows, rel_cols, cotangent, fc1_weight),
        (
            S((heads, tok, 128), BF16), S((heads, tok, 128), F32), S((tok, width), BF16), S((heads, 1, tok), F32),
            S((heads, tok, 256), BF16), S((heads, tok, 256), BF16),
            S(own, BF16), S(full, BF16), S(blocks, BF16), S((tok, D), BF16),
        ),
        [
            pltpu.VMEM((heads, tok, 128), BF16), pltpu.VMEM((128, tok), BF16), pltpu.VMEM((256, 128), BF16),
            pltpu.VMEM((256, 128), BF16), pltpu.VMEM((tok, 256), BF16),
        ]
        + swap + share + spread, hbm_in=(6,), hbm_out=(8,),
    )
    fc1_full = fc1_full.reshape(D, ff)
    mid, a2, fc2_full, act, slope, cot_turned = comm_call(
        partial(mid_kernel, shards), "mid", 2,
        (proj_part.reshape(full), x, vec, fc2_t, fc1_full, cot),
        (
            S(own, F32), S(full, BF16), S(blocks, BF16), S((tok, ff), BF16), S((tok, ff), F32),
            S((D, tok), BF16),
        ),
        gather + share + spread, hbm_in=(3,), hbm_out=(2,),
    )
    fc2_full = fc2_full.reshape(D, ff)
    d_mid, _, d_branch_turned, fc2_own, sums, fc1_grad, mlp_part, d_o = comm_call(
        partial(turn_kernel, shards), "turn", 3,
        (
            cot_turned, act, slope, cot.reshape(tok, D), fc2_full, fc1_full, a2.reshape(tok, D), mid, g, vec,
            w1_full,
        ),
        (
            S(own, F32), S(full, BF16), S((D, tok), BF16), S(block, F32), S((8, D), F32),
            S((D, ff), BF16), S((tok, D), BF16), S((tok, width), BF16),
        ),
        [pltpu.VMEM((D, ff), BF16), pltpu.VMEM(full, BF16), pltpu.VMEM((tok, ff), BF16)]
        + gather + share + collect,
    )
    dqkv, rel_grad, fc1_own, qkv_sum, output = comm_call(
        partial(bwd_kernel, shards, heads, HD, COLS, rows, 256), "attn_bwd", 4,
        (qa, ka, vh, d_o, oh, lse, rel_rows, rel_cols, fc1_grad, mlp_part.reshape(full), mid, vec),
        (S((tok, qkv_cols), BF16), S((256, 128), F32), S(block, F32), S((8, qkv_cols), F32), S(own, BF16)),
        [
            pltpu.VMEM((heads, tok, 128), BF16), pltpu.VMEM((3 * heads, tok, 128), BF16),
            pltpu.VMEM((256, tok), BF16), pltpu.VMEM((tok, 128), F32), pltpu.VMEM((tok, 128), F32),
            pltpu.VMEM((8, tok), F32), pltpu.VMEM((256, 128), BF16), pltpu.VMEM((tok, 256), BF16),
            pltpu.VMEM(own, BF16),
        ] + gather + swap + collect,
    )
    qkv_sum = qkv_sum[0]
    qv_part = jnp.stack([qkv_sum[:width], qkv_sum[2 * width :]])
    qv_placed = lax.dynamic_update_slice_in_dim(jnp.zeros((2, D), F32), qv_part, tp_rank * width, 1)
    fc1_placed = lax.dynamic_update_slice_in_dim(jnp.zeros((FF,), F32), sums[4], tp_rank * ff, 0)
    terms = (
        jnp.zeros((2 * D,), F32),
        qv_placed.reshape(-1),
        fc1_placed,
        sums[:4].reshape(-1),
        rel_grad[: rel_rows.shape[0], :HD].reshape(-1),
        rel_grad[128 : 128 + rel_cols.shape[0], :HD].reshape(-1),
    )
    count = sum(term.shape[0] for term in terms)
    lines = -(-count // (8 * D)) * 8
    packed = jnp.concatenate(terms + (jnp.zeros((lines * D - count,), F32),)).reshape(lines, D)
    tokens_grad, qkv_own, proj_own, total = comm_call(
        partial(end_kernel, shards), "end", 5,
        (x, d_mid, vec, a1_turned, dqkv, d_branch_turned, o_low, packed, w1_full),
        (S(own, BF16), S((3, block[0], width), F32), S((block[0], width), F32), S((lines, D), F32)),
        [pltpu.VMEM((D, ff), BF16), pltpu.VMEM(block, F32), pltpu.VMEM(full, BF16), pltpu.VMEM(own, BF16)]
        + gather + swap
        + [
            pltpu.VMEM((4, lines, D), F32), pltpu.VMEM((3, lines, D), F32),
            pltpu.VMEM((shards, lines, D), F32), DMA((2, 2 + shards)),
        ]
        + collect,
    )
    flat = total.reshape(-1)
    base = 4 * D + FF
    rel_at = base + 4 * D
    rel_mid = rel_at + rel_rows.size
    return (
        output,
        tokens_grad,
        total[0],
        total[1],
        qkv_own,
        total[2:4],
        flat[rel_at:rel_mid].reshape(rel_rows.shape),
        flat[rel_mid : rel_mid + rel_cols.size].reshape(rel_cols.shape),
        proj_own.T,
        flat[base + 2 * D : base + 3 * D],
        flat[base : base + D],
        flat[base + D : base + 2 * D],
        fc1_own,
        flat[4 * D : base],
        fc2_own.T,
        flat[base + 3 * D : base + 4 * D],
    )


def solution(mesh):
    in_specs = (
        P("shard", ("ctx", "tp"), None),
        P(),
        P(),
        P(None, ("shard", "ctx"), "tp"),
        P(),
        P(),
        P(),
        P("tp", ("shard", "ctx")),
        P(),
        P(),
        P(),
        P(("shard", "ctx"), "tp"),
        P(),
        P("tp", ("shard", "ctx")),
        P(),
        P("shard", ("ctx", "tp"), None),
    )
    out_specs = (
        P("shard", ("ctx", "tp"), None),
        P("shard", ("ctx", "tp"), None),
        P(),
        P(),
        P(None, ("shard", "ctx"), "tp"),
        P(),
        P(),
        P(),
        P("tp", ("shard", "ctx")),
        P(),
        P(),
        P(),
        P(("shard", "ctx"), "tp"),
        P(),
        P("tp", ("shard", "ctx")),
        P(),
    )
    def on_device(*arrays):
        rows = (arrays[5].shape[0] + 1) // 2
        fits = mesh.shape["tp"] == 4 and mesh.shape["ctx"] == 2 and HD + 2 * rows <= 128
        fits = fits and arrays[0].shape[0] == mesh.shape["ctx"] and arrays[6].shape[0] <= 128
        return (on_device_images if fits else on_device_rows)(*arrays)

    return jax.shard_map(
        on_device, mesh=mesh, in_specs=in_specs, out_specs=out_specs, check_vma=False
    )
```

profile of v0, /device:TPU:8, one launch (start us, length us, event | category | flops | bytes accessed | tf_op | source)
XLA Modules:
  0.0 339.7 jit_solution(9761823481795920008)
XLA Ops:
  0.6 0.9 dynamic-slice_reduce_fusion
  1.5 0.8 dynamic_slice.6
  2.3 0.9 concatenate.6
  3.8 47.1 %front.1 = (bf16[2,128,1280]{2,1,0:T(8,128)(2,1)}, bf16[2,4,128,1280]{3,2,1,0:T(8,128)(2,1)}, bf16[8,160,1280]{2,1,0:T(8,128)(2,1)}, bf16[1280,1024]{1,0:T(8,128)(2,1)}) custom-call(bf16[2,128,1280]{2,1,0:T(8,128)(2,1)} %tok_ref.1, bf16[3,160,320]{2,1,0:T(8,128)(2,1)} %qkvw_ref.1, bf16[160,320]{1,0:T(8,128)(2,1)} %bitcast.26, f32[8,1280]{1,0:T(8,128)} %reshape.90.vec_ref), custom_call_target="tpu_custom_call" | custom-call | tf_op jit(solution)/shard_map/front/pallas_call | solution.py:753
  50.9 1.5 copy.35.rc_ref
  52.3 52.5 %attn_fwd.1 = (bf16[4,1024,128]{2,1,0:T(8,128)(2,1)}, f32[4,1024,128]{2,1,0:T(8,128)}, bf16[1024,320]{1,0:T(8,128)(2,1)}, f32[4,1,1024]{2,1,0:T(1,128)}, bf16[4,...) custom-call(bf16[1024,1280]{1,0:T(8,128)(2,1)} %bitcast.20, ...), custom_call_target="tpu_custom_call" | custom-call | tf_op jit(solution)/shard_map/attn_fwd/pallas_call | solution.py:753
  104.9 49.0 %mid.1 = (f32[2,128,1280]{2,1,0:T(8,128)}, bf16[2,4,128,1280]{3,2,1,0:T(8,128)(2,1)}, bf16[8,160,1280]{2,1,0:T(8,128)(2,1)}, bf16[1024,1280]{1,0:T(8,128)(2,1)},...) custom-call(bf16[2,4,128,1280]{3,2,1,0:T(8,128)(2,1)} %bitcast.21, bf16[2,128,1280]{2,1,0:T(8,128)(2,1)} %get-tuple-element.58.x_ref, ...), custom_call_target="tpu_custom_call" | custom-call | tf_op jit(solution)/shard_map/mid/pallas_call | solution.py:753
  153.9 61.4 %turn.1 = (f32[2,128,1280]{2,1,0:T(8,128)}, bf16[2,4,128,1280]{3,2,1,0:T(8,128)(2,1)}, bf16[1280,1024]{1,0:T(8,128)(2,1)}, f32[160,1280]{1,0:T(8,128)}, f32[8,12...) custom-call(bf16[1280,1024]{1,0:T(8,128)(2,1)} %get-tuple-element.61.ct_ref, ...), custom_call_target="tpu_custom_call" | custom-call | tf_op jit(solution)/shard_map/turn/pallas_call | solution.py:753
  215.4 49.0 %attn_bwd.1 = (bf16[1024,960]{1,0:T(8,128)(2,1)}, f32[256,128]{1,0:T(8,128)}, f32[160,1280]{1,0:T(8,128)}, f32[8,960]{1,0:T(8,128)}, bf16[2,128,1280]{2,1,0:T(8,128)(2,1)}) custom-call(bf16[4,1024,256]{2,1,0:T(8,128)(2,1)} %get-tuple-element.54.qa_ref, bf16[4,1024,256]{2,1,0:T(8,128)(2,1)} %get-tuple-element.55.ka_ref, ...), custom_call_target="tpu_custom_call" | custom-call | tf_op jit(solution)/shard_map/attn_bwd/pallas_call | solution.py:753
  264.4 0.7 fusion
  265.3 0.8 slice.85
  266.3 0.7 slice.84
  268.5 58.0 %end.1 = (bf16[2,128,1280]{2,1,0:T(8,128)(2,1)}, f32[3,160,320]{2,1,0:T(8,128)}, f32[160,320]{1,0:T(8,128)}, f32[24,1280]{1,0:T(8,128)}) custom-call(bf16[2,128,1280]{2,1,0:T(8,128)(2,1)} %get-tuple-element.58.x_ref, f32[2,128,1280]{2,1,0:T(8,128)} %get-tuple-element.74.dm_ref, f32[8,1280]{1,0:T(8,128)} %reshape.90.vec_ref, ...), custom_call_target="tpu_custom_call" | custom-call | tf_op jit(solution)/shard_map/end/pallas_call | solution.py:753
  326.5 1.2 slice.89
  327.7 0.7 copy.37
  329.0 1.6 slice_reduce_fusion
  330.7 0.8 slice.98
  332.1 1.4 slice.88
  333.5 0.8 copy.46
  334.3 2.0 copy.47
  336.3 0.9 copy.48
  337.2 0.7 copy.49
  337.9 0.9 copy.50
  338.8 0.9 copy.51
  (32 shorter events, 3.6 us)
Async XLA Ops:
  215.3 51.7 %copy-start.5 = (f32[8,1280]{1,0:T(8,128)S(1)}, f32[8,1280]{1,0:T(8,128)}, u32[]{:S(2)}) copy-start(f32[8,1280]{1,0:T(8,128)} %get-tuple-element.80) | copy-start | bytes 122884
  268.5 65.0 %copy-start.3 = (bf16[2,128,1280]{2,1,0:T(8,128)(2,1)S(1)}, bf16[2,128,1280]{2,1,0:T(8,128)(2,1)}, u32[]{:S(2)}) copy-start(bf16[2,128,1280]{2,1,0:T(8,128)(2,1)} %get-tuple-element.130) | copy-start | bytes 1966084
  326.5 9.8 %copy-start.2 = (f32[3,160,320]{2,1,0:T(8,128)S(1)}, f32[3,160,320]{2,1,0:T(8,128)}, u32[]{:S(2)}) copy-start(f32[3,160,320]{2,1,0:T(8,128)} %get-tuple-element.134) | copy-start | bytes 1843204
  326.5 10.7 %copy-start.4 = (f32[160,320]{1,0:T(8,128)S(1)}, f32[160,320]{1,0:T(8,128)}, u32[]{:S(2)}) copy-start(f32[160,320]{1,0:T(8,128)} %get-tuple-element.85) | copy-start | bytes 614404
  326.5 11.4 %copy-start.1 = (f32[160,1280]{1,0:T(8,128)S(1)}, f32[160,1280]{1,0:T(8,128)}, u32[]{:S(2)}) copy-start(f32[160,1280]{1,0:T(8,128)} %get-tuple-element.142) | copy-start | bytes 2457604
  334.3 4.5 %copy-start = (f32[160,1280]{1,0:T(8,128)S(1)}, f32[160,1280]{1,0:T(8,128)}, u32[]{:S(2)}) copy-start(f32[160,1280]{1,0:T(8,128)} %get-tuple-element.87) | copy-start | bytes 2457604
where the time goes:
time: 342 us; the launch traced here: 340 us
  Pallas kernels  317 us (93%)
  local copies, waits for them, and re-layouts  21.7 us (6%)
    pallas_call x6, Pallas kernels, comm_call(): pl.pallas_call(kernel, out_shape=tuple(outs), in_specs=[ANY if i in hbm_i...  317 us
    unnamed x20, local copies, waits for them, and re-layouts  8.4 us

commit v1 on v0

--- a/solution.py
+++ b/solution.py
@@ -731,31 +731,64 @@
     return inverse * (scaled - first - unit * second)
 
 
-def row_tiles(out_ref, left_ref, right_ref, dims, first, count, tile=256):
-    def one(i, _):
-        at = pl.ds(pl.multiple_of(i * tile, tile), tile)
-        out_ref[at, :] = mm(left_ref[at, :], right_ref[...], dims).astype(out_ref.dtype)
-        return 0
-
-    lax.fori_loop(first, first + count, one, 0)
-
-
-def grad_tiles(out_ref, left_ref, right_ref, first, count, cols=slice(None), tile=256):
-    def one(i, _):
-        at = pl.ds(pl.multiple_of(i * tile, tile), tile)
-        out_ref[at, cols] = mm(left_ref[:, at], right_ref[...], TN).astype(out_ref.dtype)
-        return 0
-
-    lax.fori_loop(first, first + count, one, 0)
-
-
-def comm_call(kernel, name, ident, args, outs, scratch, hbm_in=(), hbm_out=()):
+class Stream:
+    def __init__(self, loads, stores, sems):
+        self.loads, self.stores, self.sems, self.flying = loads, stores, sems, []
+
+    def need(self, *operands):
+        for i in operands:
+            if i in self.loads:
+                self.loads.pop(i).wait()
+
+    def put(self, j, half=None):
+        src, dst, q = self.stores[j]
+        if half is not None:
+            size = src.shape[0] // 2
+            src, dst = src.at[half * size : (half + 1) * size], dst.at[half * size : (half + 1) * size]
+        copy = pltpu.make_async_copy(src, dst, self.sems.at[2 * q + (half or 0)])
+        copy.start()
+        self.flying.append((j, copy))
+
+    def close(self):
+        self.need(*list(self.loads))
+        done = [j for j, _ in self.flying]
+        for j in self.stores:
+            if j not in done:
+                self.put(j)
+        for _, copy in self.flying:
+            copy.wait()
+
+
+def comm_call(kernel, name, ident, args, outs, scratch, hbm_in=(), hbm_out=(), late=(), early=()):
+    count, results, own = len(args), len(outs), len(scratch)
+
+    def body(*refs):
+        ins, out = list(refs[:count]), list(refs[count : count + results])
+        inner = refs[count + results : count + results + own]
+        extra = refs[count + results + own :]
+        buffers, load_sems, store_sems = extra[:-2], extra[-2], extra[-1]
+        loads, stores = {}, {}
+        for q, i in enumerate(late):
+            loads[i] = pltpu.make_async_copy(ins[i], buffers[q], load_sems.at[q])
+            loads[i].start()
+            ins[i] = buffers[q]
+        for q, j in enumerate(early):
+            held = buffers[len(late) + q]
+            stores[j] = (held, out[j], q)
+            out[j] = held
+        stream = Stream(loads, stores, store_sems)
+        kernel(stream, *ins, *out, *inner)
+        stream.close()
+
     return pl.pallas_call(
-        kernel,
+        body,
         out_shape=tuple(outs),
-        in_specs=[ANY if i in hbm_in else VM for i in range(len(args))],
-        out_specs=tuple(ANY if i in hbm_out else VM for i in range(len(outs))),
-        scratch_shapes=scratch,
+        in_specs=[ANY if i in hbm_in or i in late else VM for i in range(count)],
+        out_specs=tuple(ANY if j in hbm_out or j in early else VM for j in range(results)),
+        scratch_shapes=list(scratch)
+        + [pltpu.VMEM(args[i].shape, args[i].dtype) for i in late]
+        + [pltpu.VMEM(outs[j].shape, outs[j].dtype) for j in early]
+        + [DMA((max(len(late), 1),)), DMA((max(2 * len(early), 1),))],
         compiler_params=pltpu.CompilerParams(
             vmem_limit_bytes=VMEM_GRANT, collective_id=ident, has_side_effects=True
         ),
@@ -775,7 +808,7 @@
 
 
 def front_kernel(
-    shards, tok_ref, qkvw_ref, pw_ref, vec_ref, x_ref, a_ref, wf_ref, at_ref,
+    shards, io, tok_ref, qkvw_ref, pw_ref, vec_ref, x_ref, a_ref, wf_ref, at_ref,
     w1_ref, swap_sems, share_sems, w_sems, w_local,
 ):
     s, c, t = place()
@@ -805,17 +838,20 @@
     spread.tick(6)
     share.finish(0, c)
     share.finish(1, 1 - c)
+    io.put(0)
+    io.put(1)
     turned(at_ref, a_ref, 0)
     spread.tick(2)
     spread.tick(4)
     turned(at_ref, a_ref, 1)
+    io.put(3)
     spread.tick(2)
     spread.tick(spread.end)
     spread.finish()
 
 
 def fwd_kernel(
-    shards, heads, hd, cols, rows, qb,
+    shards, heads, hd, cols, rows, qb, io,
     a1_ref, w1_ref, vec_ref, rr_ref, rc_ref, cot_ref, w_ref,
     vh_ref, oh_ref, ob_ref, lse_ref, qa_ref, ka_ref, g_ref, cf_ref, wf_ref, pp_ref,
     qh_ref, vt_ref, rt_ref, tab_ref, hot_ref, swap_sems, share_sems, w_sems, w_local,
@@ -838,6 +874,8 @@
     cf_ref[me, t] = own
     share.push(0, me, cot_ref.at[me])
 
+    io.need(0, 1)
+
     def project(i, _):
         at = pl.ds(pl.multiple_of(i * qb, qb), qb)
         tile = (mm(a1_ref[at, :], w1_ref[:, 0:wide]) + vec_ref[7:8, 0:wide]).astype(BF16)
@@ -853,6 +891,8 @@
         return 0
 
     lax.fori_loop(0, blocks, project, 0)
+    io.put(0)
+    io.put(5)
     swap.wait()
     cf_ref[1 - me, t] = g_ref[1 - me]
     share.push(1, 1 - me, g_ref.at[1 - me])
@@ -884,8 +924,10 @@
             l = jnp.sum(p, 0, keepdims=True)
             lse_ref[h, :, at] = m * c + jnp.log2(l)
             oh_ref[h, at, :] = (mm(vt_ref[...], p.astype(BF16)) / l).T
-            for k in range(2):
-                spread.poll(spread.first + 2 * (h * blocks + i) + k)
+            turn = h * blocks + i
+            event = spread.first + turn + (turn + 1) // 2
+            spread.poll(event)
+            pl.when(turn % 2 == 0)(lambda: spread.poll(event + 1))
             return 0
 
         lax.fori_loop(0, blocks, blk, 0)
@@ -894,35 +936,46 @@
         return 0
 
     lax.fori_loop(0, heads, head, 0)
+    io.put(1)
+    io.put(4)
     for h in range(heads):
         ob_ref[:, h * hd : (h + 1) * hd] = oh_ref[h, :, 0:hd].astype(BF16)
+
+    io.put(2)
+    done = spread.first + heads * blocks * 3 // 2
 
     def out_rows(i, _):
         at = pl.ds(pl.multiple_of(i * qb, qb), qb)
         pp_ref[at, :] = mm(ob_ref[at, :], w1_ref[:, wide:], NT).astype(BF16)
+        for k in range(2):
+            spread.poll(done + 2 * i + k)
         return 0
 
     lax.fori_loop(0, blocks, out_rows, 0)
-    spread.run(spread.first + 2 * heads * blocks, spread.end)
+    io.put(9)
+    spread.run(done + 2 * blocks, spread.end)
     share.finish(0, me)
     share.finish(1, 1 - me)
+    io.put(7)
     spread.finish()
 
 
 def mid_kernel(
-    shards, part_ref, x_ref, vec_ref, w_ref, f1_ref, cf_ref,
+    shards, io, part_ref, x_ref, vec_ref, w_ref, f1_ref, cf_ref,
     mid_ref, a_ref, wf_ref, act_ref, slope_ref, ct_ref,
     mate, far, outb, sum_sems, share_sems, w_sems, w_local,
 ):
     _, _, t = place()
     greet(shards)
     gather = Gather2(part_ref, mate, far, outb, sum_sems)
+    io.need(0)
     gather.push(0)
     gather.push(1)
     spread = Spread(shards, w_ref, wf_ref, w_sems, w_local)
     share = Share(a_ref, share_sems)
     gather.forward(0)
     gather.forward(1)
+    io.need(5, 1)
     turned(ct_ref, cf_ref, 0)
     spread.tick(8)
     for p in range(2):
@@ -933,6 +986,8 @@
         share.push(p, p)
         if p == 1:
             turned(ct_ref, cf_ref, 1)
+            io.put(0)
+            io.put(5)
         spread.tick(7)
     share.forward(0, 0)
     half = a_ref.shape[1] * a_ref.shape[2]
@@ -955,20 +1010,26 @@
         spread.now += a_ref.shape[1]
 
     share.finish(0, 0)
+    io.need(4)
     hidden(0)
+    io.put(3, 0)
+    io.put(4, 0)
     spread.tick(spread.end)
     share.forward(1, 1)
     share.finish(1, 1)
+    io.put(1)
     hidden(1)
+    io.put(4, 1)
+    io.put(3, 1)
     for p in range(2):
         gather.finish(p)
     spread.finish()
 
 
 def turn_kernel(
-    shards, ct_ref, act_ref, slope_ref, cot_ref, f2_ref, f1_ref, a2_ref, mid_ref, g_ref, vec_ref, w1_ref,
-    dm_ref, db_ref, dbt_ref, wg_ref, sums_ref, f1g_ref, mlp_ref, do_ref,
-    w2g_ref, part_ref, dp_ref, mate, far, outb, sum_sems, share_sems, w_held, w_sems,
+    shards, io, ct_ref, act_ref, slope_ref, cot_ref, f2_ref, f1_ref, a2_ref, mid_ref, g_ref, vec_ref, w1_ref,
+    dm_ref, dbt_ref, wg_ref, sums_ref, f1g_ref, mlp_ref, do_ref,
+    db_ref, w2g_ref, part_ref, dp_ref, mate, far, outb, sum_sems, share_sems, w_held, w_sems,
 ):
     _, _, t = place()
     greet(shards)
@@ -980,32 +1041,38 @@
     sums_ref[...] = jnp.zeros_like(sums_ref)
     step = collect.pieces
 
+    io.need(0, 1, 2, 3, 4, 5)
+
     def back(n, _):
         def block(j, _):
             at = collect.pair_rows(n, j)
             w2g_ref[at, :] = mm(ct_ref[at, :], act_ref[...]).astype(BF16)
             return 0
 
-        lax.fori_loop(0, 2, block, 0)
+        def blocks():
+            lax.fori_loop(0, 2, block, 0)
+
+        pl.when(n < halves)(lambda: blocks())
         pl.when(n == 0)(collect.begin)
-        pl.when(n == halves)(lambda: gather.forward(0))
         p, i = n // halves, n % halves
         at = pl.ds(pl.multiple_of(n * tile, tile), tile)
         d_pre = (mm(cot_ref[at, :], f2_ref[...]) * slope_ref[at, :]).astype(BF16)
         dp_ref[at, :] = d_pre
         sums_ref[4:5, :] += jnp.sum(d_pre.astype(F32), 0, keepdims=True)
         for k in range(2):
-            collect.poll(step * n + k)
+            collect.poll(step * n - 2 + k)
+        pl.when(n == halves)(lambda: gather.forward(0))
         d_a2 = mm(d_pre, f1_ref[...], NT).astype(BF16)
         part_ref[p, pl.ds(2 * i, 2)] = d_a2.reshape(2, tile // 2, -1)
         pl.when(n == halves - 1)(lambda: gather.push(0))
+        pl.when(n == 2 * halves - 1)(lambda: gather.push(1))
+        pl.when(n >= halves)(lambda: blocks())
         for k in range(2, step):
-            collect.poll(step * n + k)
+            collect.poll(step * n - 2 + k)
         return 0
 
     lax.fori_loop(0, 2 * halves, back, 0)
-    gather.push(1)
-    base = 2 * halves * step
+    base = 2 * halves * step - 2
 
     def hidden_grad(i, _):
         at = pl.ds(pl.multiple_of(i * 256, 256), 256)
@@ -1030,7 +1097,10 @@
         return 0
 
     count = f1g_ref.shape[0] // 256
+    io.need(6, 7, 8)
     lax.fori_loop(0, count, hidden_grad, 0)
+    io.put(0)
+    io.put(4)
     base2 = base + count
 
     def mlp(n, _):
@@ -1042,9 +1112,11 @@
         return 0
 
     lax.fori_loop(0, 2 * halves, mlp, 0)
+    io.put(5)
     collect.run(base2 + 4 * halves, collect.end)
     share.forward(1, 1)
     wide = do_ref.shape[1]
+    io.need(10)
 
     def d_o(n, _):
         p, i = n // halves, n % halves
@@ -1056,13 +1128,15 @@
         return 0
 
     lax.fori_loop(0, 2 * halves, d_o, 0)
+    io.put(1)
+    io.put(6)
     for p in range(2):
         gather.finish(p)
     collect.finish(wg_ref)
 
 
 def bwd_kernel(
-    shards, heads, hd, cols, rows, qb,
+    shards, heads, hd, cols, rows, qb, io,
     qa_ref, ka_ref, vh_ref, do_ref, oh_ref, lse_ref, rr_ref, rc_ref, w_ref, part_ref, mid_ref, vec_ref,
     dqkv_ref, rg_ref, wg_ref, qs_ref, out_ref,
     doh_ref, dh_ref, kt_ref, acc_k, acc_v, del_ref, tab_ref, hot_ref, res_ref,
@@ -1073,11 +1147,14 @@
     _, me, _ = place()
     greet(shards)
     gather = Gather2(part_ref, mate, far, outb, sum_sems)
+    io.need(9)
     gather.push(0)
     gather.push(1)
     swap = swap_copy(res_ref.at[1 - me], out_ref.at[me], swap_sems)
     collect = Collect(shards, w_ref, w_held, w_sems)
+    io.need(8)
     collect.begin()
+    io.need(3)
     tok, wide = dqkv_ref.shape
     blocks = tok // qb
     for h in range(heads):
@@ -1088,6 +1165,8 @@
     scale = hd**-0.5
     c = scale * math.log2(math.e)
     rg_ref[...] = jnp.zeros_like(rg_ref)
+
+    io.need(0, 1, 2, 4, 10)
 
     def head(h, _):
         kt_ref[0:128, :] = jnp.where(lane_ids((tok, 128)) < hd, ka_ref[h, :, 0:128], hot_ref[:, 0:128]).T
@@ -1145,6 +1224,7 @@
     out_ref[me] = res_ref[me]
     for j in range(3 * heads):
         dqkv_ref[:, j * hd : (j + 1) * hd] = dh_ref[j, :, 0:hd]
+    io.put(0)
     collect.run(collect.first + 2 * heads * blocks, collect.end)
     qs_ref[...] = mm(jnp.ones((8, tok), BF16), dqkv_ref[...])
     for p in range(2):
@@ -1154,7 +1234,7 @@
 
 
 def end_kernel(
-    shards, x_ref, dm_ref, vec_ref, at_ref, dqkv_ref, dbt_ref, ob_ref, small_ref, w1_ref,
+    shards, io, x_ref, dm_ref, vec_ref, at_ref, dqkv_ref, dbt_ref, ob_ref, small_ref, w1_ref,
     grad_ref, qg_ref, pg_ref, total_ref,
     w1g_ref, wg_ref, part_ref, gres_ref, mate, far, outb, sum_sems, swap_sems,
     held, got, line, small_sems, w_held, w_sems,
@@ -1168,15 +1248,9 @@
     halves = part_ref.shape[1] // 2
     step = collect.pieces
 
+    io.need(4, 8, 3, 5, 6)
+
     def back(n, _):
-        p, i = n // halves, n % halves
-        rows = pl.ds(pl.multiple_of(n * tile, tile), tile)
-        d_a1 = mm(dqkv_ref[rows, :], w1_ref[:, 0:wide], NT).astype(BF16)
-        part_ref[p, pl.ds(2 * i, 2)] = d_a1.reshape(2, tile // 2, -1)
-        pl.when(n == halves - 1)(lambda: gather.push(0))
-        for k in range(step):
-            collect.poll(step * (n - 1) + k)
-
         def block(j, _):
             at = collect.pair_rows(n, j)
             w1g_ref[at, 0:wide] = mm(at_ref[at, :], dqkv_ref[...]).astype(BF16)
@@ -1185,24 +1259,38 @@
 
         lax.fori_loop(0, 2, block, 0)
         pl.when(n == 0)(collect.begin)
-        pl.when(n == halves)(lambda: gather.forward(0))
+        for k in range(2):
+            collect.poll(step * n + k)
+        pl.when(n == 2)(lambda: gather.forward(1))
+
+        def rows_of(i, _):
+            rows = pl.ds(pl.multiple_of((n * halves + i) * tile, tile), tile)
+            d_a1 = mm(dqkv_ref[rows, :], w1_ref[:, 0:wide], NT).astype(BF16)
+            part_ref[n, pl.ds(2 * i, 2)] = d_a1.reshape(2, tile // 2, -1)
+            return 0
+
+        @pl.when(n < 2)
+        def _():
+            lax.fori_loop(0, halves, rows_of, 0)
+            gather.push(n)
+
+        for k in range(2, step):
+            collect.poll(step * n + k)
+        pl.when(n == 1)(lambda: gather.forward(0))
         return 0
 
     lax.fori_loop(0, 2 * halves, back, 0)
-    gather.push(1)
-    collect.now = step * (2 * halves - 1)
-    collect.tick(2)
-    gather.forward(1)
-    collect.tick(2)
+    collect.now = step * 2 * halves
     held[0] = small_ref[...]
+    io.need(0, 1)
     for p in range(2):
         unit, inverse = ln_stats(x_ref[p].astype(F32))
-        collect.tick(2)
+        collect.tick(1)
         da = gather.result(p)
         gres_ref[p] = (dm_ref[p] + ln_back(unit, inverse, vec_ref[0:1, :], da)).astype(BF16)
         held[0, 0:1, :] += jnp.sum(da * unit, 0, keepdims=True)
         held[0, 1:2, :] += jnp.sum(da, 0, keepdims=True)
-        collect.tick(3)
+        collect.tick(1)
     grad_ref[me] = gres_ref[me]
     swap = swap_copy(gres_ref.at[1 - me], grad_ref.at[me], swap_sems)
     waits = []
@@ -1235,6 +1323,19 @@
     for p in range(2):
         gather.finish(p)
     swap.wait()
+
+
+def settle_kernel(rows, *refs):
+    count = (len(refs) - 1 - len(rows)) // 2
+    total_ref = refs[count]
+    outs = refs[count + 1 :]
+    for k in range(count):
+        outs[k][...] = refs[k][...]
+    for k, (row, size) in enumerate(rows):
+        if size == 1:
+            outs[count + k][...] = total_ref[row, :]
+        else:
+            outs[count + k][...] = total_ref[row : row + size, :]
 
 
 def on_device_images(
@@ -1276,7 +1377,7 @@
         partial(front_kernel, shards), "front", 0,
         (tokens, qkv_weight, proj_weight.T, vec),
         (S(own, BF16), S(full, BF16), S(blocks, BF16), S((D, tok), BF16)),
-        [pltpu.VMEM(block, BF16)] + swap + share + spread, hbm_out=(2,),
+        [pltpu.VMEM(block, BF16)] + swap + share + spread, hbm_out=(2,), early=(0, 1, 3),
     )
     w1_full = w1_full.reshape(D, -1)
     vh, oh, o_low, lse, qa, ka, g, cot, fc1_full, proj_part = comm_call(
@@ -1291,7 +1392,7 @@
             pltpu.VMEM((heads, tok, 128), BF16), pltpu.VMEM((128, tok), BF16), pltpu.VMEM((256, 128), BF16),
             pltpu.VMEM((256, 128), BF16), pltpu.VMEM((tok, 256), BF16),
         ]
-        + swap + share + spread, hbm_in=(6,), hbm_out=(8,),
+        + swap + share + spread, hbm_in=(6,), hbm_out=(8,), late=(1, 0), early=(0, 1, 2, 4, 5, 7, 9),
     )
     fc1_full = fc1_full.reshape(D, ff)
     mid, a2, fc2_full, act, slope, cot_turned = comm_call(
@@ -1301,21 +1402,22 @@
             S(own, F32), S(full, BF16), S(blocks, BF16), S((tok, ff), BF16), S((tok, ff), F32),
             S((D, tok), BF16),
         ),
-        gather + share + spread, hbm_in=(3,), hbm_out=(2,),
+        gather + share + spread, hbm_in=(3,), hbm_out=(2,), late=(0, 5, 1, 4), early=(0, 1, 3, 4, 5),
     )
     fc2_full = fc2_full.reshape(D, ff)
-    d_mid, _, d_branch_turned, fc2_own, sums, fc1_grad, mlp_part, d_o = comm_call(
+    d_mid, d_branch_turned, fc2_own, sums, fc1_grad, mlp_part, d_o = comm_call(
         partial(turn_kernel, shards), "turn", 3,
         (
             cot_turned, act, slope, cot.reshape(tok, D), fc2_full, fc1_full, a2.reshape(tok, D), mid, g, vec,
             w1_full,
         ),
         (
-            S(own, F32), S(full, BF16), S((D, tok), BF16), S(block, F32), S((8, D), F32),
+            S(own, F32), S((D, tok), BF16), S(block, F32), S((8, D), F32),
             S((D, ff), BF16), S((tok, D), BF16), S((tok, width), BF16),
         ),
-        [pltpu.VMEM((D, ff), BF16), pltpu.VMEM(full, BF16), pltpu.VMEM((tok, ff), BF16)]
+        [pltpu.VMEM(full, BF16), pltpu.VMEM((D, ff), BF16), pltpu.VMEM(full, BF16), pltpu.VMEM((tok, ff), BF16)]
         + gather + share + collect,
+        late=(0, 1, 2, 3, 4, 5, 6, 7, 8, 10), early=(0, 1, 4, 5, 6),
     )
     dqkv, rel_grad, fc1_own, qkv_sum, output = comm_call(
         partial(bwd_kernel, shards, heads, HD, COLS, rows, 256), "attn_bwd", 4,
@@ -1327,6 +1429,7 @@
             pltpu.VMEM((8, tok), F32), pltpu.VMEM((256, 128), BF16), pltpu.VMEM((tok, 256), BF16),
             pltpu.VMEM(own, BF16),
         ] + gather + swap + collect,
+        late=(8, 9, 3, 2, 4, 1, 0, 10), early=(0,),
     )
     qkv_sum = qkv_sum[0]
     qv_part = jnp.stack([qkv_sum[:width], qkv_sum[2 * width :]])
@@ -1354,7 +1457,20 @@
             pltpu.VMEM((shards, lines, D), F32), DMA((2, 2 + shards)),
         ]
         + collect,
-    )
+        late=(4, 8, 3, 5, 6, 0, 1),
+    )
+    rows_out = 4 + FF // D
+    places = ((0, 1), (1, 1), (2, 2), (rows_out + 2, 1), (rows_out, 1), (rows_out + 1, 1), (rows_out + 3, 1))
+    big = (output, tokens_grad, qkv_own, proj_own, fc1_own, fc2_own)
+    final = pl.pallas_call(
+        partial(settle_kernel, places),
+        out_shape=tuple(S(b.shape, b.dtype) for b in big)
+        + tuple(S((D,) if size == 1 else (size, D), F32) for _, size in places),
+        compiler_params=pltpu.CompilerParams(vmem_limit_bytes=VMEM_GRANT),
+        name="settle",
+    )(*big, total)
+    output, tokens_grad, qkv_own, proj_own, fc1_own, fc2_own = final[:6]
+    gain1, bias1, qv_grad, projb, gain2, bias2, fc2b = final[6:]
     flat = total.reshape(-1)
     base = 4 * D + FF
     rel_at = base + 4 * D
@@ -1362,20 +1478,20 @@
     return (
         output,
         tokens_grad,
-        total[0],
-        total[1],
+        gain1,
+        bias1,
         qkv_own,
-        total[2:4],
+        qv_grad,
         flat[rel_at:rel_mid].reshape(rel_rows.shape),
         flat[rel_mid : rel_mid + rel_cols.size].reshape(rel_cols.shape),
         proj_own.T,
-        flat[base + 2 * D : base + 3 * D],
-        flat[base : base + D],
-        flat[base + D : base + 2 * D],
+        projb,
+        gain2,
+        bias2,
         fc1_own,
         flat[4 * D : base],
         fc2_own.T,
-        flat[base + 3 * D : base + 4 * D],
+        fc2b,
     )
 
 

time: 342 us -> 310 us (0.906)
  Pallas kernels: 317 us -> 297 us
  local copies, waits for them, and re-layouts: 21.7 us -> 10.7 us
    pallas_call x6 -> x7, Pallas kernels: 317 us -> 297 us  [the longest x6 293 us: comm_call(): pl.pallas_call(body, out_shape=tuple(outs), in_specs=[ANY if i in hbm_in...]
    unnamed x20 -> x6, local copies, waits for them, and re-layouts: 8.4 us -> 2.17 us
where the time goes in v1:
time: 310 us; the launch traced here: 309 us
  Pallas kernels  297 us (96%)
  local copies, waits for them, and re-layouts  10.7 us (3%)
    pallas_call x6, Pallas kernels, comm_call(): pl.pallas_call(body, out_shape=tuple(outs), in_specs=[ANY if i in hbm_in...  293 us

profile of v1, /device:TPU:8, one launch (start us, length us, event | category | flops | bytes accessed | tf_op | source)
XLA Modules:
  0.0 308.8 jit_solution(12681322186576893634)
XLA Ops:
  0.6 0.9 dynamic-slice_reduce_fusion
  1.5 0.8 dynamic_slice.6
  2.3 0.9 concatenate.6
  3.2 0.6 reshape.86.refs_3_.refs_2_.refs_9_.refs_11_
  3.8 44.6 %front.1 = (bf16[2,128,1280]{2,1,0:T(8,128)(2,1)}, bf16[2,4,128,1280]{3,2,1,0:T(8,128)(2,1)}, bf16[8,160,1280]{2,1,0:T(8,128)(2,1)}, bf16[1280,1024]{1,0:T(8,128)(2,1)}) custom-call(bf16[2,128,1280]{2,1,0:T(8,128)(2,1)} %refs_0_.1, bf16[3,160,320]{2,1,0:T(8,128)(2,1)} %refs_1_.1, bf16[160,320]{1,0:T(8,128)(2,1)} %bitcast.24, ...), custom_call_target="tpu_custom_call" | custom-call | tf_op jit(solution)/shard_map/front/pallas_call | solution.py:783
  48.4 1.5 copy.35.refs_4_.refs_7_
  49.9 46.2 %attn_fwd.1 = (bf16[4,1024,128]{2,1,0:T(8,128)(2,1)}, f32[4,1024,128]{2,1,0:T(8,128)}, bf16[1024,320]{1,0:T(8,128)(2,1)}, f32[4,1,1024]{2,1,0:T(1,128)}, bf16[4,...) custom-call(bf16[1024,1280]{1,0:T(8,128)(2,1)} %bitcast.20, ...), custom_call_target="tpu_custom_call" | custom-call | tf_op jit(solution)/shard_map/attn_fwd/pallas_call | solution.py:783
  96.0 43.0 %mid.1 = (f32[2,128,1280]{2,1,0:T(8,128)}, bf16[2,4,128,1280]{3,2,1,0:T(8,128)(2,1)}, bf16[8,160,1280]{2,1,0:T(8,128)(2,1)}, bf16[1024,1280]{1,0:T(8,128)(2,1)},...) custom-call(bf16[2,4,128,1280]{3,2,1,0:T(8,128)(2,1)} %bitcast.21, ...), custom_call_target="tpu_custom_call" | custom-call | tf_op jit(solution)/shard_map/mid/pallas_call | solution.py:783
  139.1 54.7 %turn.1 = (f32[2,128,1280]{2,1,0:T(8,128)}, bf16[1280,1024]{1,0:T(8,128)(2,1)}, f32[160,1280]{1,0:T(8,128)}, f32[8,1280]{1,0:T(8,128)}, bf16[1280,1280]{1,0:T(8,...) custom-call(bf16[1280,1024]{1,0:T(8,128)(2,1)} %get-tuple-element.74.refs_0_, ...), custom_call_target="tpu_custom_call" | custom-call | tf_op jit(solution)/shard_map/turn/pallas_call | solution.py:783
  193.8 45.6 %attn_bwd.1 = (bf16[1024,960]{1,0:T(8,128)(2,1)}, f32[256,128]{1,0:T(8,128)}, f32[160,1280]{1,0:T(8,128)}, f32[8,960]{1,0:T(8,128)}, bf16[2,128,1280]{2,1,0:T(8,128)(2,1)}) custom-call(bf16[4,1024,256]{2,1,0:T(8,128)(2,1)} %get-tuple-element.67.refs_0_, bf16[4,1024,256]{2,1,0:T(8,128)(2,1)} %get-tuple-element.68.refs_1_, ...), custom_call_target="tpu_custom_call" | custom-call | tf_op jit(solution)/shard_map/attn_bwd/pallas_call | solution.py:783
  239.4 0.8 slice.52
  240.2 0.1 reshape.98
  240.3 0.7 fusion
  241.1 0.4 dynamic_update_slice.6
  241.5 0.7 slice.51
  242.3 0.3 dynamic_update_slice.7
  242.7 0.1 concatenate.7
  242.8 0.7 reshape.99.refs_7_
  243.5 59.0 %end.1 = (bf16[2,128,1280]{2,1,0:T(8,128)(2,1)}, f32[3,160,320]{2,1,0:T(8,128)}, f32[160,320]{1,0:T(8,128)}, f32[24,1280]{1,0:T(8,128)}) custom-call(bf16[2,128,1280]{2,1,0:T(8,128)(2,1)} %get-tuple-element.71.refs_1_.refs_0_, f32[2,128,1280]{2,1,0:T(8,128)} %get-tuple-element.87.refs_1_, f32[8,1280]{1,0:T(8,128)} %reshape.86.refs_3_.refs_2_.refs_9_.refs_11_, ...), custom_call_target="tpu_custom_call" | custom-call | tf_op jit(solution)/shard_map/end/pallas_call | solution.py:783
  302.5 4.1 %settle.1 = (bf16[2,128,1280]{2,1,0:T(8,128)(2,1)}, bf16[2,128,1280]{2,1,0:T(8,128)(2,1)}, f32[3,160,320]{2,1,0:T(8,128)}, f32[160,320]{1,0:T(8,128)}, f32[160,1...) custom-call(bf16[2,128,1280]{2,1,0:T(8,128)(2,1)} %get-tuple-element, ...), custom_call_target="tpu_custom_call" | custom-call | tf_op jit(solution)/shard_map/settle/pallas_call | solution.py:1465
  306.7 0.1 slice.53
  306.9 0.7 copy.37
  307.6 0.6 slice.58
  308.2 0.6 slice.57
  (17 shorter events, 0.2 us)
Async XLA Ops:
  193.7 48.5 %copy-start.1 = (f32[8,1280]{1,0:T(8,128)S(1)}, f32[8,1280]{1,0:T(8,128)}, u32[]{:S(2)}) copy-start(f32[8,1280]{1,0:T(8,128)} %get-tuple-element.93) | copy-start | bytes 122884
  302.5 4.2 %copy-start = (f32[24,1280]{1,0:T(8,128)S(1)}, f32[24,1280]{1,0:T(8,128)}, u32[]{:S(2)}) copy-start(f32[24,1280]{1,0:T(8,128)} %get-tuple-element.100.refs_6_) | copy-start | bytes 368644

commit v2 on v1

--- a/solution.py
+++ b/solution.py
@@ -467,7 +467,10 @@
         back = to // shards
         peers.append({"shard": to * (1 - back) + (size - 1 - to) * back, "ctx": back})
     if line:
-        peers += [{"shard": lax.rem(s + d, shards)} for d in range(1, shards)]
+        peers.append({"tp": core_mate(far_mate(t))})
+        for d in range(1, shards):
+            peers.append({"shard": lax.rem(s + d, shards)})
+            peers.append({"shard": lax.rem(s + d, shards), "ctx": 1 - c})
     barrier = pltpu.get_barrier_semaphore()
     for peer in peers:
         pl.semaphore_signal(barrier, inc=1, device_id=peer, device_id_type=pl.DeviceIdType.MESH)
@@ -1234,13 +1237,51 @@
 
 
 def end_kernel(
-    shards, io, x_ref, dm_ref, vec_ref, at_ref, dqkv_ref, dbt_ref, ob_ref, small_ref, w1_ref,
-    grad_ref, qg_ref, pg_ref, total_ref,
+    shards, io, x_ref, dm_ref, vec_ref, at_ref, dqkv_ref, dbt_ref, ob_ref, sums_ref, w1_ref, rg_ref, qs_ref,
+    grad_ref, qg_ref, pg_ref, total_ref, late_ref,
     w1g_ref, wg_ref, part_ref, gres_ref, mate, far, outb, sum_sems, swap_sems,
-    held, got, line, small_sems, w_held, w_sems,
+    held, got, line, small_sems, near, wide_all, late_sems, w_held, w_sems,
 ):
     s, me, t = place()
+    half = held.shape[2] // 2
+    held[0] = jnp.zeros_like(held[0])
+    held[0, :, 0:128] = rg_ref[0:32, :]
+    for k in range(4):
+        held[0, :, 128 * (k + 1) : 128 * (k + 2)] = rg_ref[128 + 32 * k : 160 + 32 * k, :]
+    for k in range(4):
+        for u in range(2):
+            held[0, 2 * k + u : 2 * k + u + 1, half:] = sums_ref[k : k + 1, u * half : (u + 1) * half]
+    for u in range(2):
+        held[0, pl.ds(8 + 2 * t + u, 1), half:] = sums_ref[4:5, u * half : (u + 1) * half]
+    span = dqkv_ref.shape[1] // 3
+    pair = jnp.concatenate([qs_ref[0:1, 0:span], qs_ref[0:1, 2 * span :]], 1)
+    held[0, pl.ds(16 + t, 1), half:] = pair
+    mine = pl.ds(pl.multiple_of(8 * t, 8), 8)
+    mates = ({"tp": core_mate(t)}, {"tp": far_mate(t)}, {"tp": core_mate(far_mate(t))})
+
+    def whole(k):
+        return aim(held.at[k], got.at[k], small_sems, k, mates[k])
+
+    def cross():
+        return aim(held.at[2, mine], got.at[2, mine], small_sems, 2, {"ctx": 1 - me})
+
+    def along(d):
+        return aim(held.at[3, mine], line.at[s], small_sems, 2 + d, {"shard": lax.rem(s + d, shards)})
+
+    def spread_sum(k):
+        return aim(total_ref.at[mine], total_ref.at[mine], small_sems, 2 + shards + k, mates[k])
+
+    def close_by(k):
+        return aim(near.at[t], near.at[t], late_sems, k, mates[k])
+
+    def far_off(d, flip):
+        there = {"shard": lax.rem(s + d, shards), "ctx": 1 - me if flip else me}
+        own = wide_all.at[2 * s + me]
+        return aim(own, own, late_sems, 3 + 2 * d + flip, there)
+
+    others = [(d, flip) for d in range(shards) for flip in range(2) if d + flip > 0]
     greet(shards, True)
+    whole(0).start()
     gather = Gather2(part_ref, mate, far, outb, sum_sems)
     collect = Collect(shards, w1g_ref, w_held, w_sems)
     wide = dqkv_ref.shape[1]
@@ -1277,65 +1318,117 @@
         for k in range(2, step):
             collect.poll(step * n + k)
         pl.when(n == 1)(lambda: gather.forward(0))
+
+        @pl.when(n == 0)
+        def _():
+            whole(0).wait_recv()
+            held[1] = held[0] + got[0]
+            whole(1).start()
+
+        @pl.when(n == 1)
+        def _():
+            whole(1).wait_recv()
+            held[2] = held[1] + got[1]
+            cross().start()
+
+        @pl.when(n == 2)
+        def _():
+            cross().wait_recv()
+            held[3, mine] = held[2, mine] + got[2, mine]
+            line[s] = held[3, mine]
+            for d in range(1, shards):
+                along(d).start()
+
         return 0
 
     lax.fori_loop(0, 2 * halves, back, 0)
     collect.now = step * 2 * halves
-    held[0] = small_ref[...]
     io.need(0, 1)
+    first = jnp.zeros((1, x_ref.shape[2]), F32)
+    second = jnp.zeros((1, x_ref.shape[2]), F32)
     for p in range(2):
         unit, inverse = ln_stats(x_ref[p].astype(F32))
         collect.tick(1)
         da = gather.result(p)
         gres_ref[p] = (dm_ref[p] + ln_back(unit, inverse, vec_ref[0:1, :], da)).astype(BF16)
-        held[0, 0:1, :] += jnp.sum(da * unit, 0, keepdims=True)
-        held[0, 1:2, :] += jnp.sum(da, 0, keepdims=True)
+        first = first + jnp.sum(da * unit, 0, keepdims=True)
+        second = second + jnp.sum(da, 0, keepdims=True)
         collect.tick(1)
+    for k in range(4):
+        near[t, k : k + 1, :] = first[:, k * span : (k + 1) * span]
+        near[t, 4 + k : 5 + k, :] = second[:, k * span : (k + 1) * span]
+    for k in range(3):
+        close_by(k).start()
     grad_ref[me] = gres_ref[me]
     swap = swap_copy(gres_ref.at[1 - me], grad_ref.at[me], swap_sems)
-    waits = []
-    for k, peer in enumerate(({"tp": core_mate(t)}, {"tp": far_mate(t)}, {"ctx": 1 - me})):
-        copy = send(held.at[k], got.at[k], small_sems, k, peer)
-        if k == 2:
-            swap.start()
-        collect.tick(2)
-        copy.wait_recv()
-        waits.append(copy)
-        held[k + 1] = held[k] + got[k]
-    line[s] = held[3]
     for d in range(1, shards):
-        waits.append(send(held.at[3], line.at[s], small_sems, 2 + d, {"shard": lax.rem(s + d, shards)}))
+        along(d).wait_recv()
+    acc = line[0]
+    for k in range(1, shards):
+        acc = acc + line[k]
+    total_ref[mine] = acc
+    for k in range(3):
+        spread_sum(k).start()
+    collect.tick(2)
+    for k in range(3):
+        close_by(k).wait_recv()
+    wide_all[2 * s + me] = near[0] + near[1] + near[2] + near[3]
+    for d, flip in others:
+        far_off(d, flip).start()
+    swap.start()
     collect.tick(collect.end)
     collect.finish(wg_ref)
     part = wide // 3
     for j in range(3):
         qg_ref[j] = wg_ref[:, j * part : (j + 1) * part]
     pg_ref[...] = wg_ref[:, wide:]
-    for k, copy in enumerate(waits):
-        if k < 3:
-            copy.wait_send()
-        else:
-            copy.wait()
-    acc = line[0]
-    for k in range(1, shards):
-        acc = acc + line[k]
-    total_ref[...] = acc
+    for d, flip in others:
+        far_off(d, flip).wait()
+    acc = wide_all[0]
+    for k in range(1, 2 * shards):
+        acc = acc + wide_all[k]
+    late_ref[...] = acc
+    for k in range(3):
+        spread_sum(k).wait()
+        close_by(k).wait_send()
+    for k in range(2):
+        whole(k).wait_send()
+    cross().wait_send()
+    for d in range(1, shards):
+        along(d).wait_send()
     for p in range(2):
         gather.finish(p)
     swap.wait()
 
 
-def settle_kernel(rows, *refs):
-    count = (len(refs) - 1 - len(rows)) // 2
-    total_ref = refs[count]
-    outs = refs[count + 1 :]
-    for k in range(count):
-        outs[k][...] = refs[k][...]
-    for k, (row, size) in enumerate(rows):
-        if size == 1:
-            outs[count + k][...] = total_ref[row, :]
-        else:
-            outs[count + k][...] = total_ref[row : row + size, :]
+def settle_kernel(
+    total_ref, late_ref, out_ref, grad_ref, qg_ref, pg_ref, f1_ref, f2_ref,
+    out_to, grad_to, qg_to, pg_to, f1_to, f2_to,
+    gain1_to, bias1_to, qv_to, rr_to, rc_to, gain2_to, bias2_to, projb_to, fc2b_to, fc1b_to,
+):
+    for here, there in (
+        (out_ref, out_to), (grad_ref, grad_to), (qg_ref, qg_to), (pg_ref, pg_to), (f1_ref, f1_to), (f2_ref, f2_to)
+    ):
+        there[...] = here[...]
+    half = total_ref.shape[1] // 2
+    span = late_ref.shape[1]
+
+    def side(parts):
+        return jnp.concatenate(parts, 1)
+
+    gain1_to[...] = side([late_ref[k : k + 1, :] for k in range(4)])[0, :]
+    bias1_to[...] = side([late_ref[4 + k : 5 + k, :] for k in range(4)])[0, :]
+    for u in range(2):
+        at = slice(half + u * span, half + (u + 1) * span)
+        qv_to[u : u + 1, :] = side([total_ref[16 + k : 17 + k, at] for k in range(4)])
+    rr_to[...] = total_ref[0 : rr_to.shape[0], 0 : rr_to.shape[1]]
+    for k in range(4):
+        size = min(32, rc_to.shape[0] - 32 * k)
+        rc_to[32 * k : 32 * k + size, :] = total_ref[0:size, 128 * (k + 1) : 128 * (k + 1) + rc_to.shape[1]]
+    for k, there in enumerate((gain2_to, bias2_to, projb_to, fc2b_to)):
+        there[...] = side([total_ref[2 * k + u : 2 * k + u + 1, half:] for u in range(2)])[0, :]
+    for k in range(4):
+        fc1b_to[k : k + 1, :] = side([total_ref[8 + 2 * k + u : 9 + 2 * k + u, half:] for u in range(2)])
 
 
 def on_device_images(
@@ -1431,67 +1524,38 @@
         ] + gather + swap + collect,
         late=(8, 9, 3, 2, 4, 1, 0, 10), early=(0,),
     )
-    qkv_sum = qkv_sum[0]
-    qv_part = jnp.stack([qkv_sum[:width], qkv_sum[2 * width :]])
-    qv_placed = lax.dynamic_update_slice_in_dim(jnp.zeros((2, D), F32), qv_part, tp_rank * width, 1)
-    fc1_placed = lax.dynamic_update_slice_in_dim(jnp.zeros((FF,), F32), sums[4], tp_rank * ff, 0)
-    terms = (
-        jnp.zeros((2 * D,), F32),
-        qv_placed.reshape(-1),
-        fc1_placed,
-        sums[:4].reshape(-1),
-        rel_grad[: rel_rows.shape[0], :HD].reshape(-1),
-        rel_grad[128 : 128 + rel_cols.shape[0], :HD].reshape(-1),
-    )
-    count = sum(term.shape[0] for term in terms)
-    lines = -(-count // (8 * D)) * 8
-    packed = jnp.concatenate(terms + (jnp.zeros((lines * D - count,), F32),)).reshape(lines, D)
-    tokens_grad, qkv_own, proj_own, total = comm_call(
+    tokens_grad, qkv_own, proj_own, total, late = comm_call(
         partial(end_kernel, shards), "end", 5,
-        (x, d_mid, vec, a1_turned, dqkv, d_branch_turned, o_low, packed, w1_full),
-        (S(own, BF16), S((3, block[0], width), F32), S((block[0], width), F32), S((lines, D), F32)),
+        (x, d_mid, vec, a1_turned, dqkv, d_branch_turned, o_low, sums, w1_full, rel_grad, qkv_sum),
+        (
+            S(own, BF16), S((3, block[0], width), F32), S((block[0], width), F32), S((32, D), F32), S((8, width), F32),
+        ),
         [pltpu.VMEM((D, ff), BF16), pltpu.VMEM(block, F32), pltpu.VMEM(full, BF16), pltpu.VMEM(own, BF16)]
         + gather + swap
         + [
-            pltpu.VMEM((4, lines, D), F32), pltpu.VMEM((3, lines, D), F32),
-            pltpu.VMEM((shards, lines, D), F32), DMA((2, 2 + shards)),
+            pltpu.VMEM((4, 32, D), F32), pltpu.VMEM((3, 32, D), F32),
+            pltpu.VMEM((shards, 8, D), F32), DMA((2, 5 + shards)),
+            pltpu.VMEM((4, 8, width), F32), pltpu.VMEM((2 * shards, 8, width), F32), DMA((2, 3 + 2 * shards)),
         ]
         + collect,
         late=(4, 8, 3, 5, 6, 0, 1),
     )
-    rows_out = 4 + FF // D
-    places = ((0, 1), (1, 1), (2, 2), (rows_out + 2, 1), (rows_out, 1), (rows_out + 1, 1), (rows_out + 3, 1))
     big = (output, tokens_grad, qkv_own, proj_own, fc1_own, fc2_own)
-    final = pl.pallas_call(
-        partial(settle_kernel, places),
+    vector = S((D,), F32)
+    (
+        output, tokens_grad, qkv_own, proj_own, fc1_own, fc2_own,
+        gain1, bias1, qv_grad, rows_grad, cols_grad, gain2, bias2, projb, fc2b, fc1b,
+    ) = pl.pallas_call(
+        settle_kernel,
         out_shape=tuple(S(b.shape, b.dtype) for b in big)
-        + tuple(S((D,) if size == 1 else (size, D), F32) for _, size in places),
+        + (vector, vector, S((2, D), F32), S(rel_rows.shape, F32), S(rel_cols.shape, F32))
+        + (vector, vector, vector, vector, S((tp_count, ff), F32)),
         compiler_params=pltpu.CompilerParams(vmem_limit_bytes=VMEM_GRANT),
         name="settle",
-    )(*big, total)
-    output, tokens_grad, qkv_own, proj_own, fc1_own, fc2_own = final[:6]
-    gain1, bias1, qv_grad, projb, gain2, bias2, fc2b = final[6:]
-    flat = total.reshape(-1)
-    base = 4 * D + FF
-    rel_at = base + 4 * D
-    rel_mid = rel_at + rel_rows.size
+    )(total, late, *big)
     return (
-        output,
-        tokens_grad,
-        gain1,
-        bias1,
-        qkv_own,
-        qv_grad,
-        flat[rel_at:rel_mid].reshape(rel_rows.shape),
-        flat[rel_mid : rel_mid + rel_cols.size].reshape(rel_cols.shape),
-        proj_own.T,
-        projb,
-        gain2,
-        bias2,
-        fc1_own,
-        flat[4 * D : base],
-        fc2_own.T,
-        fc2b,
+        output, tokens_grad, gain1, bias1, qkv_own, qv_grad, rows_grad, cols_grad, proj_own.T, projb,
+        gain2, bias2, fc1_own, fc1b.reshape(FF), fc2_own.T, fc2b,
     )
 
 
@@ -1534,8 +1598,9 @@
     )
     def on_device(*arrays):
         rows = (arrays[5].shape[0] + 1) // 2
-        fits = mesh.shape["tp"] == 4 and mesh.shape["ctx"] == 2 and HD + 2 * rows <= 128
-        fits = fits and arrays[0].shape[0] == mesh.shape["ctx"] and arrays[6].shape[0] <= 128
+        fits = (mesh.shape["shard"], mesh.shape["ctx"], mesh.shape["tp"]) == (4, 2, 4)
+        fits = fits and arrays[0].shape[0] == mesh.shape["ctx"] and HD + 2 * rows <= 128
+        fits = fits and arrays[5].shape[0] <= 32 and arrays[6].shape[0] <= 128
         return (on_device_images if fits else on_device_rows)(*arrays)
 
     return jax.shard_map(

time: 310 us -> 303 us (0.977)
  Pallas kernels: 297 us -> 291 us
  local copies, waits for them, and re-layouts: 10.7 us -> 7.48 us
    pallas_call x6, Pallas kernels: 293 us -> 287 us  [comm_call(): pl.pallas_call(body, out_shape=tuple(outs), in_specs=[ANY if i in hbm_in...]
    slice x10 -> x0, local copies, waits for them, and re-layouts: 3.69 us -> none  [the longest x1 0.85 us: on_device_images(): rel_grad[128:128 + rel_cols.shape[0], :HD].reshape(-1)]
where the time goes in v2:
time: 303 us; the launch traced here: 299 us
  Pallas kernels  291 us (96%)
  local copies, waits for them, and re-layouts  7.48 us (2%)
    pallas_call x6, Pallas kernels, comm_call(): pl.pallas_call(body, out_shape=tuple(outs), in_specs=[ANY if i in hbm_in...  287 us

profile of v2, /device:TPU:8, one launch (start us, length us, event | category | flops | bytes accessed | tf_op | source)
XLA Modules:
  0.0 299.1 jit_solution(12557043862784661443)
XLA Ops:
  0.7 0.9 dynamic-slice_reduce_fusion
  1.5 0.8 dynamic_slice.6
  2.3 0.9 concatenate.3
  3.2 0.6 reshape.62.refs_3_.refs_2_.refs_9_.refs_11_
  3.8 1.5 copy.32.refs_4_.refs_7_
  5.2 44.6 %front.1 = (bf16[2,128,1280]{2,1,0:T(8,128)(2,1)}, bf16[2,4,128,1280]{3,2,1,0:T(8,128)(2,1)}, bf16[8,160,1280]{2,1,0:T(8,128)(2,1)}, bf16[1280,1024]{1,0:T(8,128)(2,1)}) custom-call(bf16[2,128,1280]{2,1,0:T(8,128)(2,1)} %refs_0_.1, bf16[3,160,320]{2,1,0:T(8,128)(2,1)} %refs_1_.1, bf16[160,320]{1,0:T(8,128)(2,1)} %bitcast.24, ...), custom_call_target="tpu_custom_call" | custom-call | tf_op jit(solution)/shard_map/front/pallas_call | solution.py:786
  49.9 46.2 %attn_fwd.1 = (bf16[4,1024,128]{2,1,0:T(8,128)(2,1)}, f32[4,1024,128]{2,1,0:T(8,128)}, bf16[1024,320]{1,0:T(8,128)(2,1)}, f32[4,1,1024]{2,1,0:T(1,128)}, bf16[4,...) custom-call(bf16[1024,1280]{1,0:T(8,128)(2,1)} %bitcast.20, ...), custom_call_target="tpu_custom_call" | custom-call | tf_op jit(solution)/shard_map/attn_fwd/pallas_call | solution.py:786
  96.1 43.0 %mid.1 = (f32[2,128,1280]{2,1,0:T(8,128)}, bf16[2,4,128,1280]{3,2,1,0:T(8,128)(2,1)}, bf16[8,160,1280]{2,1,0:T(8,128)(2,1)}, bf16[1024,1280]{1,0:T(8,128)(2,1)},...) custom-call(bf16[2,4,128,1280]{3,2,1,0:T(8,128)(2,1)} %bitcast.21, ...), custom_call_target="tpu_custom_call" | custom-call | tf_op jit(solution)/shard_map/mid/pallas_call | solution.py:786
  139.1 54.7 %turn.1 = (f32[2,128,1280]{2,1,0:T(8,128)}, bf16[1280,1024]{1,0:T(8,128)(2,1)}, f32[160,1280]{1,0:T(8,128)}, f32[8,1280]{1,0:T(8,128)}, bf16[1280,1280]{1,0:T(8,...) custom-call(bf16[1280,1024]{1,0:T(8,128)(2,1)} %get-tuple-element.75.refs_0_, ...), custom_call_target="tpu_custom_call" | custom-call | tf_op jit(solution)/shard_map/turn/pallas_call | solution.py:786
  193.8 45.6 %attn_bwd.1 = (bf16[1024,960]{1,0:T(8,128)(2,1)}, f32[256,128]{1,0:T(8,128)}, f32[160,1280]{1,0:T(8,128)}, f32[8,960]{1,0:T(8,128)}, bf16[2,128,1280]{2,1,0:T(8,128)(2,1)}) custom-call(bf16[4,1024,256]{2,1,0:T(8,128)(2,1)} %get-tuple-element.84.refs_0_, bf16[4,1024,256]{2,1,0:T(8,128)(2,1)} %get-tuple-element.85.refs_1_, ...), custom_call_target="tpu_custom_call" | custom-call | tf_op jit(solution)/shard_map/attn_bwd/pallas_call | solution.py:786
  239.3 52.7 %end.1 = (bf16[2,128,1280]{2,1,0:T(8,128)(2,1)}, f32[3,160,320]{2,1,0:T(8,128)}, f32[160,320]{1,0:T(8,128)}, f32[32,1280]{1,0:T(8,128)}, f32[8,320]{1,0:T(8,128)}) custom-call(bf16[2,128,1280]{2,1,0:T(8,128)(2,1)} %get-tuple-element.69.refs_1_.refs_0_, f32[2,128,1280]{2,1,0:T(8,128)} %get-tuple-element.82.refs_1_, ...), custom_call_target="tpu_custom_call" | custom-call | tf_op jit(solution)/shard_map/end/pallas_call | solution.py:786
  292.0 4.2 %settle.1 = (bf16[2,128,1280]{2,1,0:T(8,128)(2,1)}, bf16[2,128,1280]{2,1,0:T(8,128)(2,1)}, f32[3,160,320]{2,1,0:T(8,128)}, f32[160,320]{1,0:T(8,128)}, f32[160,1...) custom-call(f32[32,1280]{1,0:T(8,128)} %get-tuple-element.98.total_r, ...), custom_call_target="tpu_custom_call" | custom-call | tf_op jit(solution)/shard_map/settle/pallas_call | solution.py:1548
  296.2 1.3 reshape.71
  297.6 1.5 copy.34
  (1 shorter events, 0.0 us)

commit v3 on v2

--- a/solution.py
+++ b/solution.py
@@ -436,7 +436,9 @@
 def fill_tables(tab_ref, rr_ref, rc_ref):
     tab_ref[...] = jnp.zeros_like(tab_ref)
     tab_ref[0 : rr_ref.shape[0], 0 : rr_ref.shape[1]] = rr_ref[...]
-    tab_ref[128 : 128 + rc_ref.shape[0], 0 : rc_ref.shape[1]] = rc_ref[...]
+    wide = jnp.concatenate([rc_ref[...], jnp.zeros((rc_ref.shape[0], 128 - rc_ref.shape[1]), BF16)], 1)
+    square = jnp.concatenate([wide, jnp.zeros((128 - rc_ref.shape[0], 128), BF16)], 0)
+    tab_ref[128:256, :] = square.T
 
 
 def fill_hots(hot_ref, hd, cols, rows, second):
@@ -1044,7 +1046,16 @@
     sums_ref[...] = jnp.zeros_like(sums_ref)
     step = collect.pieces
 
-    io.need(0, 1, 2, 3, 4, 5)
+    io.need(0, 1)
+
+    def first(j, _):
+        at = collect.pair_rows(0, j)
+        w2g_ref[at, :] = mm(ct_ref[at, :], act_ref[...]).astype(BF16)
+        return 0
+
+    lax.fori_loop(0, 2, first, 0)
+    collect.begin()
+    io.need(2, 3, 4, 5)
 
     def back(n, _):
         def block(j, _):
@@ -1055,8 +1066,7 @@
         def blocks():
             lax.fori_loop(0, 2, block, 0)
 
-        pl.when(n < halves)(lambda: blocks())
-        pl.when(n == 0)(collect.begin)
+        pl.when((n > 0) & (n < halves))(lambda: blocks())
         p, i = n // halves, n % halves
         at = pl.ds(pl.multiple_of(n * tile, tile), tile)
         d_pre = (mm(cot_ref[at, :], f2_ref[...]) * slope_ref[at, :]).astype(BF16)
@@ -1422,13 +1432,11 @@
         at = slice(half + u * span, half + (u + 1) * span)
         qv_to[u : u + 1, :] = side([total_ref[16 + k : 17 + k, at] for k in range(4)])
     rr_to[...] = total_ref[0 : rr_to.shape[0], 0 : rr_to.shape[1]]
-    for k in range(4):
-        size = min(32, rc_to.shape[0] - 32 * k)
-        rc_to[32 * k : 32 * k + size, :] = total_ref[0:size, 128 * (k + 1) : 128 * (k + 1) + rc_to.shape[1]]
+    square = jnp.concatenate([total_ref[:, 128 * (k + 1) : 128 * (k + 2)] for k in range(4)], 0).T
+    rc_to[...] = square[0 : rc_to.shape[0], 0 : rc_to.shape[1]]
     for k, there in enumerate((gain2_to, bias2_to, projb_to, fc2b_to)):
         there[...] = side([total_ref[2 * k + u : 2 * k + u + 1, half:] for u in range(2)])[0, :]
-    for k in range(4):
-        fc1b_to[k : k + 1, :] = side([total_ref[8 + 2 * k + u : 9 + 2 * k + u, half:] for u in range(2)])
+    fc1b_to[...] = side([total_ref[8 + k : 9 + k, half:] for k in range(8)])[0, :]
 
 
 def on_device_images(
@@ -1475,7 +1483,7 @@
     w1_full = w1_full.reshape(D, -1)
     vh, oh, o_low, lse, qa, ka, g, cot, fc1_full, proj_part = comm_call(
         partial(fwd_kernel, shards, heads, HD, COLS, rows, 256), "attn_fwd", 1,
-        (a1.reshape(tok, D), w1_full, vec, rel_rows, rel_cols, cotangent, fc1_weight),
+        (a1.reshape(tok, D), w1_full, vec, rel_rows, rel_cols.T, cotangent, fc1_weight),
         (
             S((heads, tok, 128), BF16), S((heads, tok, 128), F32), S((tok, width), BF16), S((heads, 1, tok), F32),
             S((heads, tok, 256), BF16), S((heads, tok, 256), BF16),
@@ -1514,7 +1522,7 @@
     )
     dqkv, rel_grad, fc1_own, qkv_sum, output = comm_call(
         partial(bwd_kernel, shards, heads, HD, COLS, rows, 256), "attn_bwd", 4,
-        (qa, ka, vh, d_o, oh, lse, rel_rows, rel_cols, fc1_grad, mlp_part.reshape(full), mid, vec),
+        (qa, ka, vh, d_o, oh, lse, rel_rows, rel_cols.T, fc1_grad, mlp_part.reshape(full), mid, vec),
         (S((tok, qkv_cols), BF16), S((256, 128), F32), S(block, F32), S((8, qkv_cols), F32), S(own, BF16)),
         [
             pltpu.VMEM((heads, tok, 128), BF16), pltpu.VMEM((3 * heads, tok, 128), BF16),
@@ -1548,14 +1556,14 @@
     ) = pl.pallas_call(
         settle_kernel,
         out_shape=tuple(S(b.shape, b.dtype) for b in big)
-        + (vector, vector, S((2, D), F32), S(rel_rows.shape, F32), S(rel_cols.shape, F32))
-        + (vector, vector, vector, vector, S((tp_count, ff), F32)),
+        + (vector, vector, S((2, D), F32), S(rel_rows.shape, F32), S(rel_cols.shape[::-1], F32))
+        + (vector, vector, vector, vector, S((FF,), F32)),
         compiler_params=pltpu.CompilerParams(vmem_limit_bytes=VMEM_GRANT),
         name="settle",
     )(total, late, *big)
     return (
-        output, tokens_grad, gain1, bias1, qkv_own, qv_grad, rows_grad, cols_grad, proj_own.T, projb,
-        gain2, bias2, fc1_own, fc1b.reshape(FF), fc2_own.T, fc2b,
+        output, tokens_grad, gain1, bias1, qkv_own, qv_grad, rows_grad, cols_grad.T, proj_own.T, projb,
+        gain2, bias2, fc1_own, fc1b, fc2_own.T, fc2b,
     )
 
 

time: 303 us -> 297 us (0.980)
  local copies, waits for them, and re-layouts: 7.48 us -> 3.13 us
where the time goes in v3:
time: 297 us; the launch traced here: 294 us
  Pallas kernels  290 us (98%)
  local copies, waits for them, and re-layouts  3.13 us (1%)
    pallas_call x6, Pallas kernels, comm_call(): pl.pallas_call(body, out_shape=tuple(outs), in_specs=[ANY if i in hbm_in...  286 us

profile of v3, /device:TPU:8, one launch (start us, length us, event | category | flops | bytes accessed | tf_op | source)
XLA Modules:
  0.0 293.7 jit_solution(3389401413071184691)
XLA Ops:
  0.6 0.9 dynamic-slice_reduce_fusion
  1.5 0.8 dynamic_slice.6
  2.3 0.9 concatenate.3
  3.2 0.6 reshape.59.refs_3_.refs_2_.refs_9_.refs_11_
  3.8 44.6 %front.1 = (bf16[2,128,1280]{2,1,0:T(8,128)(2,1)}, bf16[2,4,128,1280]{3,2,1,0:T(8,128)(2,1)}, bf16[8,160,1280]{2,1,0:T(8,128)(2,1)}, bf16[1280,1024]{1,0:T(8,128)(2,1)}) custom-call(bf16[2,128,1280]{2,1,0:T(8,128)(2,1)} %refs_0_.1, bf16[3,160,320]{2,1,0:T(8,128)(2,1)} %refs_1_.1, bf16[160,320]{1,0:T(8,128)(2,1)} %bitcast.26, ...), custom_call_target="tpu_custom_call" | custom-call | tf_op jit(solution)/shard_map/front/pallas_call | solution.py:788
  48.4 46.2 %attn_fwd.1 = (bf16[4,1024,128]{2,1,0:T(8,128)(2,1)}, f32[4,1024,128]{2,1,0:T(8,128)}, bf16[1024,320]{1,0:T(8,128)(2,1)}, f32[4,1,1024]{2,1,0:T(1,128)}, bf16[4,...) custom-call(bf16[1024,1280]{1,0:T(8,128)(2,1)} %bitcast.23, ...), custom_call_target="tpu_custom_call" | custom-call | tf_op jit(solution)/shard_map/attn_fwd/pallas_call | solution.py:788
  94.7 43.0 %mid.1 = (f32[2,128,1280]{2,1,0:T(8,128)}, bf16[2,4,128,1280]{3,2,1,0:T(8,128)(2,1)}, bf16[8,160,1280]{2,1,0:T(8,128)(2,1)}, bf16[1024,1280]{1,0:T(8,128)(2,1)},...) custom-call(bf16[2,4,128,1280]{3,2,1,0:T(8,128)(2,1)} %bitcast.24, ...), custom_call_target="tpu_custom_call" | custom-call | tf_op jit(solution)/shard_map/mid/pallas_call | solution.py:788
  137.7 53.4 %turn.1 = (f32[2,128,1280]{2,1,0:T(8,128)}, bf16[1280,1024]{1,0:T(8,128)(2,1)}, f32[160,1280]{1,0:T(8,128)}, f32[8,1280]{1,0:T(8,128)}, bf16[1280,1280]{1,0:T(8,...) custom-call(bf16[1280,1024]{1,0:T(8,128)(2,1)} %get-tuple-element.75.refs_0_, ...), custom_call_target="tpu_custom_call" | custom-call | tf_op jit(solution)/shard_map/turn/pallas_call | solution.py:788
  191.1 45.6 %attn_bwd.1 = (bf16[1024,960]{1,0:T(8,128)(2,1)}, f32[256,128]{1,0:T(8,128)}, f32[160,1280]{1,0:T(8,128)}, f32[8,960]{1,0:T(8,128)}, bf16[2,128,1280]{2,1,0:T(8,128)(2,1)}) custom-call(bf16[4,1024,256]{2,1,0:T(8,128)(2,1)} %get-tuple-element.84.refs_0_, bf16[4,1024,256]{2,1,0:T(8,128)(2,1)} %get-tuple-element.85.refs_1_, ...), custom_call_target="tpu_custom_call" | custom-call | tf_op jit(solution)/shard_map/attn_bwd/pallas_call | solution.py:788
  236.6 52.7 %end.1 = (bf16[2,128,1280]{2,1,0:T(8,128)(2,1)}, f32[3,160,320]{2,1,0:T(8,128)}, f32[160,320]{1,0:T(8,128)}, f32[32,1280]{1,0:T(8,128)}, f32[8,320]{1,0:T(8,128)}) custom-call(bf16[2,128,1280]{2,1,0:T(8,128)(2,1)} %get-tuple-element.69.refs_1_.refs_0_, f32[2,128,1280]{2,1,0:T(8,128)} %get-tuple-element.82.refs_1_, ...), custom_call_target="tpu_custom_call" | custom-call | tf_op jit(solution)/shard_map/end/pallas_call | solution.py:788
  289.3 4.2 %settle.1 = (bf16[2,128,1280]{2,1,0:T(8,128)(2,1)}, bf16[2,128,1280]{2,1,0:T(8,128)(2,1)}, f32[3,160,320]{2,1,0:T(8,128)}, f32[160,320]{1,0:T(8,128)}, f32[160,1...) custom-call(f32[32,1280]{1,0:T(8,128)} %get-tuple-element.98.total_r, ...), custom_call_target="tpu_custom_call" | custom-call | tf_op jit(solution)/shard_map/settle/pallas_call | solution.py:1556
  (1 shorter events, 0.0 us)
